TPU v7x, 128 devices: a whole 4x4x4 slice. The times are simulated.
128 devices in a mesh: section: 8 (over x, core), tp: 16 (over z, y).
Axes of the slice: x: 4, y: 4, z: 4, core: 2. Of those that a mesh axis runs over, the one named last changes fastest.
Arguments:
- pending_activation: bfloat16 [8, 128, 4096], P('section'), may hold values from -6 to 6
- admissible_microbatches: bfloat16 [4, 128, 4096], P(None, None, 'tp'), may hold values from -6 to 6
- arrival_plan: int32 [4], replicated, may hold values from 0 to 3, each once
- vanished_hop: int32 [1], replicated, may hold values from 1 to 7
- query_key_value_matrices: bfloat16 [8, 4096, 3, 2048], P('section', None, None, 'tp')
- mixing_projection_matrices: bfloat16 [8, 2048, 4096], P('section', 'tp'), may hold values from -0.125 to 0.125
- normalizer_factors: bfloat16 [8, 4096], P('section'), may hold values from 0.25 to 1.75
Outputs:
- activation_later: bfloat16 [8, 128, 4096], P('section')
- standby_input: bfloat16 [8, 128, 4096], P('section', None, 'tp')
Inputs may be any that keep to these rules, and one draw needn't show every extreme that they name: `vanished_hop`: the preempted section is not the first. `arrival_plan`: each micro-batch index once.
All inputs are finite; a program needn't handle non-finite values.
Results may differ from a plain program's by a relative error of at most 0.013.
Values may be sent and summed in bfloat16 or wider, within the bound.
A program may use at most 64 MiB of HBM per device.

v0:
```python
import jax
import jax.numpy as jnp
from jax import lax
from jax.sharding import PartitionSpec as P

HD = 128
TICKS = 3


NORM_EPS = 1e-05


def shifted(value, axis, steps):
    count = lax.axis_size(axis)
    pairs = [(source, (source + steps) % count) for source in range(count)]
    return lax.ppermute(value, axis, pairs)


def cut_along(array, dim, count):
    dims = array.shape
    blocks = array.reshape(*dims[:dim], count, dims[dim] // count, *dims[dim + 1 :])
    return jnp.moveaxis(blocks, dim, 0)


def sum_at_owner(array, axis, dim):
    blocks = cut_along(array, dim, lax.axis_size(axis))
    arrived = lax.all_to_all(blocks, axis, split_axis=0, concat_axis=0, tiled=True)
    return arrived.sum(axis=0)


def from_everyone(array, axis):
    copies = jnp.broadcast_to(array, (lax.axis_size(axis), *array.shape))
    return lax.all_to_all(copies, axis, split_axis=0, concat_axis=0, tiled=True)


def in_order(blocks, dim):
    blocks = jnp.moveaxis(blocks, 0, dim)
    dims = blocks.shape
    return blocks.reshape(*dims[:dim], dims[dim] * dims[dim + 1], *dims[dim + 2 :])


def gather_directly(array, axis, dim):
    blocks = from_everyone(array, axis)
    return in_order(blocks, dim)


def layer_norm(x_rows, scale_row):
    widened = x_rows.astype(jnp.float32)
    row_mean = jnp.mean(widened, axis=-1, keepdims=True)
    centered = widened - row_mean
    row_var = jnp.mean(centered * centered, axis=-1, keepdims=True)
    return (centered * lax.rsqrt(row_var + NORM_EPS) * scale_row.astype(jnp.float32)).astype(
        jnp.bfloat16
    )


def attend(normed, w_in, w_out):
    row_count = normed.shape[0]
    col_count = w_in.shape[2]
    head_count = col_count // HD
    projected = jnp.dot(
        normed, w_in.reshape(w_in.shape[0], 3 * col_count), preferred_element_type=jnp.float32
    )
    projected = projected.astype(jnp.bfloat16).reshape(row_count, 3, head_count, HD)
    queries = projected[:, 0]
    key_rows = projected[:, 1]
    values = projected[:, 2]
    scores = jnp.einsum(
        "qhd,khd->hqk", queries, key_rows, preferred_element_type=jnp.float32
    ) * HD ** (-0.5)
    causal = jnp.arange(row_count)[:, None] >= jnp.arange(row_count)[None, :]
    scores = jnp.where(causal[None], scores, -jnp.inf)
    row_max = jnp.max(scores, axis=-1, keepdims=True)
    weights = jnp.exp(scores - row_max)
    probs = (weights / jnp.sum(weights, axis=-1, keepdims=True)).astype(jnp.bfloat16)
    context = jnp.einsum("hqk,khd->qhd", probs, values, preferred_element_type=jnp.float32)
    context = context.astype(jnp.bfloat16).reshape(row_count, col_count)
    return jnp.dot(context, w_out, preferred_element_type=jnp.float32)


def per_device(
    pending_activation,
    admissible_microbatches,
    arrival_plan,
    vanished_hop,
    query_key_value_matrices,
    mixing_projection_matrices,
    normalizer_factors,
):
    sections = lax.axis_size("section")
    my_section = lax.axis_index("section")
    sharding_degree = lax.axis_size("tp")
    slice_breadth = pending_activation.shape[2] // sharding_degree
    col_start = lax.axis_index("tp") * slice_breadth
    lost_at = vanished_hop[0]
    is_pred = my_section == lost_at - 1
    is_next = my_section == lost_at + 1
    is_lost = my_section == lost_at
    w_in = query_key_value_matrices[0]
    w_out = mixing_projection_matrices[0]
    scale_row = normalizer_factors[0]
    entire_source_lines = pending_activation[0]
    x_sh = lax.dynamic_slice_in_dim(entire_source_lines, col_start, slice_breadth, 1)
    blank = jnp.zeros(entire_source_lines.shape, jnp.float32)
    far_in, far_out, far_gain = shifted((w_in, w_out, scale_row), "section", -1)

    def successor_layer(rows_full):
        return attend(layer_norm(rows_full, far_gain), far_in, far_out)

    standby_sh = x_sh
    for tick_index in range(TICKS):
        own_part = attend(layer_norm(entire_source_lines, scale_row), w_in, w_out)
        ya_sh = (x_sh.astype(jnp.float32) + sum_at_owner(own_part, "tp", 1)).astype(jnp.bfloat16)
        ya_full = gather_directly(ya_sh, "tp", 1)
        spare_part = (
            successor_layer(ya_full)
            if tick_index == TICKS - 1
            else lax.cond(is_pred, lambda: successor_layer(ya_full), lambda: blank)
        )
        spare_sh = (ya_sh.astype(jnp.float32) + sum_at_owner(spare_part, "tp", 1)).astype(
            jnp.bfloat16
        )
        result_sh = jnp.where(is_pred, spare_sh, ya_sh)
        entering = lax.dynamic_index_in_dim(
            admissible_microbatches, arrival_plan[tick_index], 0, keepdims=False
        )
        send_sh = jnp.where(my_section == sections - 1, entering, result_sh)
        near_rows = shifted(send_sh, "section", 1)
        far_rows = shifted(spare_sh, "section", 2)
        x_sh = jnp.where(is_lost, jnp.zeros_like(far_rows), jnp.where(is_next, far_rows, near_rows))
        entire_source_lines = gather_directly(x_sh, "tp", 1)
        standby_sh = far_rows
    return (entire_source_lines[None], standby_sh[None])


def solution(mesh):
    placed = (
        P("section", None, None),
        P(None, None, "tp"),
        P(),
        P(),
        P("section", None, None, "tp"),
        P("section", "tp", None),
        P("section", None),
    )
    return jax.shard_map(
        per_device,
        mesh=mesh,
        in_specs=placed,
        out_specs=(P("section", None, None), P("section", None, "tp")),
        check_vma=False,
    )
```

profile of v0, /device:TPU:1, one launch (start us, length us, event | category | flops | bytes accessed | tf_op | source)
XLA Modules:
  0.0 417.3 jit_solution(17218985801988183069)
XLA Ops:
  0.6 3.2 copy.102
  13.3 8.6 %all-to-all-start = ((f32[16,128,256]{2,1,0:T(8,128)}), f32[16,128,256]{2,1,0:T(8,128)}, u32[]{:S(2)}, u32[]{:S(2)}) async-start(f32[16,128,256]{2,1,0:T(8,128)} %convolution_bitcast_fusion.3), calls=%async_computation | async-start | bytes 4194304 | tf_op jit(solution)/shard_map/all_to_all | solution.py:27
  24.9 28.1 %all-to-all-done = f32[16,128,256]{2,1,0:T(8,128)} async-done(((f32[16,128,256]{2,1,0:T(8,128)}), f32[16,128,256]{2,1,0:T(8,128)}, u32[]{:S(2)}, u32[]{:S(2)}) %all-to-all-start) | async-done | bytes 2097184 | tf_op jit(solution)/shard_map/all_to_all | solution.py:27
  56.7 4.3 %all-to-all-start.1 = ((bf16[16,128,256]{2,1,0:T(8,128)(2,1)}), bf16[16,128,256]{2,1,0:T(8,128)(2,1)}, u32[]{:S(2)}, u32[]{:S(2)}) async-start(bf16[16,128,256]{2,1,0:T(8,128)(2,1)} %broadcast_in_dim.42), calls=%async_computation.1 | async-start | bytes 2097152 | tf_op jit(solution)/shard_map/all_to_all | solution.py:33
  63.5 7.4 %collective-permute-done = bf16[4096]{0:T(1024)(128)(2,1)S(1)} collective-permute-done((bf16[4096]{0:T(1024)(128)(2,1)S(1)}, bf16[4096]{0:T(1024)(128)(2,1)S(1)}, u32[]{:S(2)}, u32[]{:S(2)}) %collective-permute-start) | collective-permute-done | bytes 8224 | tf_op jit(solution)/shard_map/ppermute | solution.py:16
  70.9 5.4 %all-to-all-done.1 = bf16[16,128,256]{2,1,0:T(8,128)(2,1)} async-done(((bf16[16,128,256]{2,1,0:T(8,128)(2,1)}), bf16[16,128,256]{2,1,0:T(8,128)(2,1)}, u32[]{:S(2)}, u32[]{:S(2)}) %all-to-all-start.1) | async-done | bytes 1048608 | tf_op jit(solution)/shard_map/all_to_all | solution.py:33
  80.9 2.9 copy.112
  83.8 5.1 %all-to-all-start.2 = ((f32[16,128,256]{2,1,0:T(8,128)}), f32[16,128,256]{2,1,0:T(8,128)}, u32[]{:S(2)}, u32[]{:S(2)}) async-start(f32[16,128,256]{2,1,0:T(8,128)} %copy.112), calls=%async_computation.2 | async-start | bytes 4194304 | tf_op jit(solution)/shard_map/all_to_all | solution.py:27
  91.4 17.8 %all-to-all-done.2 = f32[16,128,256]{2,1,0:T(8,128)} async-done(((f32[16,128,256]{2,1,0:T(8,128)}), f32[16,128,256]{2,1,0:T(8,128)}, u32[]{:S(2)}, u32[]{:S(2)}) %all-to-all-start.2) | async-done | bytes 2097184 | tf_op jit(solution)/shard_map/all_to_all | solution.py:27
  111.8 6.9 %collective-permute-start.3 = (bf16[128,256]{1,0:T(8,128)(2,1)S(1)}, bf16[128,256]{1,0:T(8,128)(2,1)S(1)}, u32[]{:S(2)}, u32[]{:S(2)}) collective-permute-start(bf16[128,256]{1,0:T(8,128)(2,1)S(1)} %get-tuple-element.57), channel_id=1, source_target_pairs={{0,32},{16,48},{32,64},{48,80},{64,96},{80,112},{96,0},{112,16},{1... | collective-permute-start | bytes 196616 | tf_op jit(solution)/shard_map/ppermute | solution.py:16
  118.7 6.9 %collective-permute-start.4 = (bf16[128,256]{1,0:T(8,128)(2,1)S(1)}, bf16[128,256]{1,0:T(8,128)(2,1)S(1)}, u32[]{:S(2)}, u32[]{:S(2)}) collective-permute-start(bf16[128,256]{1,0:T(8,128)(2,1)S(1)} %get-tuple-element.56), channel_id=1, source_target_pairs={{0,16},{16,32},{32,48},{48,64},{64,80},{80,96},{96,112},{112,0},{1... | collective-permute-start | bytes 196616 | tf_op jit(solution)/shard_map/ppermute | solution.py:16
  128.2 4.5 %all-to-all-start.3 = ((bf16[16,128,256]{1,2,0:T(8,128)(2,1)}), bf16[16,128,256]{1,2,0:T(8,128)(2,1)}, u32[]{:S(2)}, u32[]{:S(2)}) async-start(bf16[16,128,256]{1,2,0:T(8,128)(2,1)} %broadcast_in_dim.43), calls=%async_computation.3 | async-start | bytes 2097152 | tf_op jit(solution)/shard_map/all_to_all | solution.py:33
  132.8 13.2 %all-to-all-done.3 = bf16[16,128,256]{1,2,0:T(8,128)(2,1)} async-done(((bf16[16,128,256]{1,2,0:T(8,128)(2,1)}), bf16[16,128,256]{1,2,0:T(8,128)(2,1)}, u32[]{:S(2)}, u32[]{:S(2)}) %all-to-all-start.3) | async-done | bytes 1048608 | tf_op jit(solution)/shard_map/all_to_all | solution.py:33
  153.0 3.2 convolution_bitcast_fusion.2
  156.2 27.8 %all_to_all.60 = f32[16,128,256]{2,1,0:T(8,128)} all-to-all(f32[16,128,256]{2,1,0:T(8,128)} %convolution_bitcast_fusion.2), channel_id=1, replica_groups=mesh['section'=8,'tp'=16] {'tp'}, dimensions={0} | all-to-all | bytes 4194304 | tf_op jit(solution)/shard_map/all_to_all | solution.py:27
  186.9 4.3 %all-to-all-start.5 = ((bf16[16,128,256]{2,1,0:T(8,128)(2,1)}), bf16[16,128,256]{2,1,0:T(8,128)(2,1)}, u32[]{:S(2)}, u32[]{:S(2)}) async-start(bf16[16,128,256]{2,1,0:T(8,128)(2,1)} %broadcast_in_dim.44), calls=%async_computation.5 | async-start | bytes 2097152 | tf_op jit(solution)/shard_map/all_to_all | solution.py:33
  191.2 12.6 %all-to-all-done.5 = bf16[16,128,256]{2,1,0:T(8,128)(2,1)} async-done(((bf16[16,128,256]{2,1,0:T(8,128)(2,1)}), bf16[16,128,256]{2,1,0:T(8,128)(2,1)}, u32[]{:S(2)}, u32[]{:S(2)}) %all-to-all-start.5) | async-done | bytes 1048608 | tf_op jit(solution)/shard_map/all_to_all | solution.py:33
  208.3 2.9 copy.122
  211.3 4.4 %all-to-all-start.6 = ((f32[16,128,256]{2,1,0:T(8,128)}), f32[16,128,256]{2,1,0:T(8,128)}, u32[]{:S(2)}, u32[]{:S(2)}) async-start(f32[16,128,256]{2,1,0:T(8,128)} %copy.122), calls=%async_computation.6 | async-start | bytes 4194304 | tf_op jit(solution)/shard_map/all_to_all | solution.py:27
  217.6 18.0 %all-to-all-done.6 = f32[16,128,256]{2,1,0:T(8,128)} async-done(((f32[16,128,256]{2,1,0:T(8,128)}), f32[16,128,256]{2,1,0:T(8,128)}, u32[]{:S(2)}, u32[]{:S(2)}) %all-to-all-start.6) | async-done | bytes 2097184 | tf_op jit(solution)/shard_map/all_to_all | solution.py:27
  238.1 9.7 %collective-permute-start.5 = (bf16[128,256]{1,0:T(8,128)(2,1)S(1)}, bf16[128,256]{1,0:T(8,128)(2,1)S(1)}, u32[]{:S(2)}, u32[]{:S(2)}) collective-permute-start(bf16[128,256]{1,0:T(8,128)(2,1)S(1)} %get-tuple-element.55), channel_id=1, source_target_pairs={{0,32},{16,48},{32,64},{48,80},{64,96},{80,112},{96,0},{112,16},{1... | collective-permute-start | bytes 196616 | tf_op jit(solution)/shard_map/ppermute | solution.py:16
  247.8 19.8 %collective-permute-start.6 = (bf16[128,256]{1,0:T(8,128)(2,1)S(1)}, bf16[128,256]{1,0:T(8,128)(2,1)S(1)}, u32[]{:S(2)}, u32[]{:S(2)}) collective-permute-start(bf16[128,256]{1,0:T(8,128)(2,1)S(1)} %get-tuple-element.54), channel_id=1, source_target_pairs={{0,16},{16,32},{32,48},{48,64},{64,80},{80,96},{96,112},{112,0},{1... | collective-permute-start | bytes 196616 | tf_op jit(solution)/shard_map/ppermute | solution.py:16
  269.3 14.6 %all_to_all.61 = bf16[16,128,256]{1,2,0:T(8,128)(2,1)S(1)} all-to-all(bf16[16,128,256]{1,2,0:T(8,128)(2,1)S(1)} %broadcast_in_dim.45), channel_id=1, replica_groups=mesh['section'=8,'tp'=16] {'tp'}, dimensions={0} | all-to-all | bytes 2097152 | tf_op jit(solution)/shard_map/all_to_all | solution.py:33
  287.3 3.2 convolution_bitcast_fusion.1
  290.5 29.0 %all_to_all.62 = f32[16,128,256]{2,1,0:T(8,128)} all-to-all(f32[16,128,256]{2,1,0:T(8,128)} %convolution_bitcast_fusion.1), channel_id=1, replica_groups=mesh['section'=8,'tp'=16] {'tp'}, dimensions={0} | all-to-all | bytes 4194304 | tf_op jit(solution)/shard_map/all_to_all | solution.py:27
  322.6 4.3 %all-to-all-start.9 = ((bf16[16,128,256]{1,2,0:T(8,128)(2,1)}), bf16[16,128,256]{1,2,0:T(8,128)(2,1)}, u32[]{:S(2)}, u32[]{:S(2)}) async-start(bf16[16,128,256]{1,2,0:T(8,128)(2,1)} %broadcast_in_dim.46), calls=%async_computation.9 | async-start | bytes 2097152 | tf_op jit(solution)/shard_map/all_to_all | solution.py:33
  329.3 12.7 %all-to-all-done.9 = bf16[16,128,256]{1,2,0:T(8,128)(2,1)} async-done(((bf16[16,128,256]{1,2,0:T(8,128)(2,1)}), bf16[16,128,256]{1,2,0:T(8,128)(2,1)}, u32[]{:S(2)}, u32[]{:S(2)}) %all-to-all-start.9) | async-done | bytes 1048608 | tf_op jit(solution)/shard_map/all_to_all | solution.py:33
  348.8 3.2 convolution_bitcast_fusion
  352.0 3.7 all-to-all-start.10
  357.7 30.6 %all-to-all-done.10 = f32[16,128,256]{2,1,0:T(8,128)S(1)} async-done(((f32[16,128,256]{2,1,0:T(8,128)}), f32[16,128,256]{2,1,0:T(8,128)S(1)}, u32[]{:S(2)}, u32[]{:S(2)}) %all-to-all-start.10) | async-done | bytes 2097184 | tf_op jit(solution)/shard_map/all_to_all | solution.py:27
  395.5 3.7 all-to-all-start.11
  399.1 15.5 %all-to-all-done.11 = bf16[16,128,256]{2,1,0:T(8,128)(2,1)S(1)} async-done(((bf16[16,128,256]{2,1,0:T(8,128)(2,1)}), bf16[16,128,256]{2,1,0:T(8,128)(2,1)S(1)}, u32[]{:S(2)}, u32[]{:S(2)}) %all-to-all-start.11) | async-done | bytes 1048608 | tf_op jit(solution)/shard_map/all_to_all | solution.py:33
  (103 shorter events, 75.3 us)
Async XLA Ops:
  0.6 3.2 copy-start.5
  3.9 5.5 %copy-start = (bf16[1,4096,3,128]{1,3,2,0:T(8,128)(2,1)}, bf16[1,4096,3,128]{1,3,2,0:T(8,128)(2,1)S(1)}, u32[]{:S(2)}) copy-start(bf16[1,4096,3,128]{1,3,2,0:T(8,128)(2,1)S(1)} %copy.102) | copy-start | bytes 9437188
  3.9 4.3 %copy-start.4 = (bf16[1,128,4096]{2,1,0:T(8,128)(2,1)S(1)}, bf16[1,128,4096]{2,1,0:T(8,128)(2,1)}, u32[]{:S(2)}) copy-start(bf16[1,128,4096]{2,1,0:T(8,128)(2,1)} %param.11) | copy-start | bytes 3145732
  11.3 2.0 copy-start.3
  13.3 39.7 %all-to-all-start = ((f32[16,128,256]{2,1,0:T(8,128)}), f32[16,128,256]{2,1,0:T(8,128)}, u32[]{:S(2)}, u32[]{:S(2)}) async-start(f32[16,128,256]{2,1,0:T(8,128)} %convolution_bitcast_fusion.3), calls=%async_computation | async-start | bytes 4194304 | tf_op jit(solution)/shard_map/all_to_all | solution.py:27
  22.0 54.3 %collective-permute-start.1 = (bf16[4096,3,128]{0,2,1:T(8,128)(2,1)}, bf16[4096,3,128]{0,2,1:T(8,128)(2,1)S(1)}, u32[]{:S(2)}, u32[]{:S(2)}) collective-permute-start(bf16[4096,3,128]{0,2,1:T(8,128)(2,1)} %bitcast.257), channel_id=1, source_target_pairs={{0,112},{16,0},{32,16},{48,32},{64,48},{80,64},{96,80},{112,96},{1... | collective-permute-start | bytes 9437192 | tf_op jit(solution)/shard_map/ppermute | solution.py:16
  23.0 48.0 %collective-permute-start.2 = (bf16[128,4096]{1,0:T(8,128)(2,1)}, bf16[128,4096]{1,0:T(8,128)(2,1)}, u32[]{:S(2)}, u32[]{:S(2)}) collective-permute-start(bf16[128,4096]{1,0:T(8,128)(2,1)} %bitcast.275), channel_id=1, source_target_pairs={{0,112},{16,0},{32,16},{48,32},{64,48},{80,64},{96,80},{112,96},{1... | collective-permute-start | bytes 3145736 | tf_op jit(solution)/shard_map/ppermute | solution.py:16
  56.7 19.6 %all-to-all-start.1 = ((bf16[16,128,256]{2,1,0:T(8,128)(2,1)}), bf16[16,128,256]{2,1,0:T(8,128)(2,1)}, u32[]{:S(2)}, u32[]{:S(2)}) async-start(bf16[16,128,256]{2,1,0:T(8,128)(2,1)} %broadcast_in_dim.42), calls=%async_computation.1 | async-start | bytes 2097152 | tf_op jit(solution)/shard_map/all_to_all | solution.py:33
  61.1 9.9 %collective-permute-start = (bf16[4096]{0:T(1024)(128)(2,1)S(1)}, bf16[4096]{0:T(1024)(128)(2,1)S(1)}, u32[]{:S(2)}, u32[]{:S(2)}) collective-permute-start(bf16[4096]{0:T(1024)(128)(2,1)S(1)} %get-tuple-element.62), channel_id=1, source_target_pairs={{0,112},{16,0},{32,16},{48,32},{64,48},{80,64},{96,80},{112,96},{1... | collective-permute-start | bytes 24584 | tf_op jit(solution)/shard_map/ppermute | solution.py:16
  83.8 5.1 %copy-start.6 = (s32[4]{0:T(128)S(1)}, s32[4]{0:T(128)}, u32[]{:S(2)}) copy-start(s32[4]{0:T(128)} %param.13) | copy-start | bytes 52
  83.8 25.4 %all-to-all-start.2 = ((f32[16,128,256]{2,1,0:T(8,128)}), f32[16,128,256]{2,1,0:T(8,128)}, u32[]{:S(2)}, u32[]{:S(2)}) async-start(f32[16,128,256]{2,1,0:T(8,128)} %copy.112), calls=%async_computation.2 | async-start | bytes 4194304 | tf_op jit(solution)/shard_map/all_to_all | solution.py:27
  111.8 13.8 %collective-permute-start.3 = (bf16[128,256]{1,0:T(8,128)(2,1)S(1)}, bf16[128,256]{1,0:T(8,128)(2,1)S(1)}, u32[]{:S(2)}, u32[]{:S(2)}) collective-permute-start(bf16[128,256]{1,0:T(8,128)(2,1)S(1)} %get-tuple-element.57), channel_id=1, source_target_pairs={{0,32},{16,48},{32,64},{48,80},{64,96},{80,112},{96,0},{112,16},{1... | collective-permute-start | bytes 196616 | tf_op jit(solution)/shard_map/ppermute | solution.py:16
  118.7 8.2 %collective-permute-start.4 = (bf16[128,256]{1,0:T(8,128)(2,1)S(1)}, bf16[128,256]{1,0:T(8,128)(2,1)S(1)}, u32[]{:S(2)}, u32[]{:S(2)}) collective-permute-start(bf16[128,256]{1,0:T(8,128)(2,1)S(1)} %get-tuple-element.56), channel_id=1, source_target_pairs={{0,16},{16,32},{32,48},{48,64},{64,80},{80,96},{96,112},{112,0},{1... | collective-permute-start | bytes 196616 | tf_op jit(solution)/shard_map/ppermute | solution.py:16
  128.2 17.8 %all-to-all-start.3 = ((bf16[16,128,256]{1,2,0:T(8,128)(2,1)}), bf16[16,128,256]{1,2,0:T(8,128)(2,1)}, u32[]{:S(2)}, u32[]{:S(2)}) async-start(bf16[16,128,256]{1,2,0:T(8,128)(2,1)} %broadcast_in_dim.43), calls=%async_computation.3 | async-start | bytes 2097152 | tf_op jit(solution)/shard_map/all_to_all | solution.py:33
  146.0 5.5 %copy-start.1 = (bf16[1,4096,3,128]{1,3,2,0:T(8,128)(2,1)S(1)}, bf16[1,4096,3,128]{1,3,2,0:T(8,128)(2,1)}, u32[]{:S(2)}) copy-start(bf16[1,4096,3,128]{1,3,2,0:T(8,128)(2,1)} %copy-done) | copy-start | bytes 9437188
  186.9 16.9 %all-to-all-start.5 = ((bf16[16,128,256]{2,1,0:T(8,128)(2,1)}), bf16[16,128,256]{2,1,0:T(8,128)(2,1)}, u32[]{:S(2)}, u32[]{:S(2)}) async-start(bf16[16,128,256]{2,1,0:T(8,128)(2,1)} %broadcast_in_dim.44), calls=%async_computation.5 | async-start | bytes 2097152 | tf_op jit(solution)/shard_map/all_to_all | solution.py:33
  211.3 24.3 %all-to-all-start.6 = ((f32[16,128,256]{2,1,0:T(8,128)}), f32[16,128,256]{2,1,0:T(8,128)}, u32[]{:S(2)}, u32[]{:S(2)}) async-start(f32[16,128,256]{2,1,0:T(8,128)} %copy.122), calls=%async_computation.6 | async-start | bytes 4194304 | tf_op jit(solution)/shard_map/all_to_all | solution.py:27
  238.1 29.5 %collective-permute-start.5 = (bf16[128,256]{1,0:T(8,128)(2,1)S(1)}, bf16[128,256]{1,0:T(8,128)(2,1)S(1)}, u32[]{:S(2)}, u32[]{:S(2)}) collective-permute-start(bf16[128,256]{1,0:T(8,128)(2,1)S(1)} %get-tuple-element.55), channel_id=1, source_target_pairs={{0,32},{16,48},{32,64},{48,80},{64,96},{80,112},{96,0},{112,16},{1... | collective-permute-start | bytes 196616 | tf_op jit(solution)/shard_map/ppermute | solution.py:16
  247.8 21.2 %collective-permute-start.6 = (bf16[128,256]{1,0:T(8,128)(2,1)S(1)}, bf16[128,256]{1,0:T(8,128)(2,1)S(1)}, u32[]{:S(2)}, u32[]{:S(2)}) collective-permute-start(bf16[128,256]{1,0:T(8,128)(2,1)S(1)} %get-tuple-element.54), channel_id=1, source_target_pairs={{0,16},{16,32},{32,48},{48,64},{64,80},{80,96},{96,112},{112,0},{1... | collective-permute-start | bytes 196616 | tf_op jit(solution)/shard_map/ppermute | solution.py:16
  283.9 1.9 copy-start.2
  322.6 19.3 %all-to-all-start.9 = ((bf16[16,128,256]{1,2,0:T(8,128)(2,1)}), bf16[16,128,256]{1,2,0:T(8,128)(2,1)}, u32[]{:S(2)}, u32[]{:S(2)}) async-start(bf16[16,128,256]{1,2,0:T(8,128)(2,1)} %broadcast_in_dim.46), calls=%async_computation.9 | async-start | bytes 2097152 | tf_op jit(solution)/shard_map/all_to_all | solution.py:33
  352.0 36.2 %all-to-all-start.10 = ((f32[16,128,256]{2,1,0:T(8,128)}), f32[16,128,256]{2,1,0:T(8,128)S(1)}, u32[]{:S(2)}, u32[]{:S(2)}) async-start(f32[16,128,256]{2,1,0:T(8,128)} %convolution_bitcast_fusion), calls=%async_computation.10 | async-start | bytes 4194304 | tf_op jit(solution)/shard_map/all_to_all | solution.py:27
  389.2 5.1 %collective-permute-start.7 = (bf16[128,256]{1,0:T(8,128)(2,1)S(1)}, bf16[128,256]{1,0:T(8,128)(2,1)S(1)}, u32[]{:S(2)}, u32[]{:S(2)}) collective-permute-start(bf16[128,256]{1,0:T(8,128)(2,1)S(1)} %get-tuple-element.53), channel_id=1, source_target_pairs={{0,32},{16,48},{32,64},{48,80},{64,96},{80,112},{96,0},{112,16},{1... | collective-permute-start | bytes 196616 | tf_op jit(solution)/shard_map/ppermute | solution.py:16
  389.3 5.1 %collective-permute-start.8 = (bf16[128,256]{1,0:T(8,128)(2,1)S(1)}, bf16[128,256]{1,0:T(8,128)(2,1)S(1)}, u32[]{:S(2)}, u32[]{:S(2)}) collective-permute-start(bf16[128,256]{1,0:T(8,128)(2,1)S(1)} %get-tuple-element.52), channel_id=1, source_target_pairs={{0,16},{16,32},{32,48},{48,64},{64,80},{80,96},{96,112},{112,0},{1... | collective-permute-start | bytes 196616 | tf_op jit(solution)/shard_map/ppermute | solution.py:16
  395.5 19.2 %all-to-all-start.11 = ((bf16[16,128,256]{2,1,0:T(8,128)(2,1)}), bf16[16,128,256]{2,1,0:T(8,128)(2,1)S(1)}, u32[]{:S(2)}, u32[]{:S(2)}) async-start(bf16[16,128,256]{2,1,0:T(8,128)(2,1)} %broadcast_in_dim.47), calls=%async_computation.11 | async-start | bytes 2097152 | tf_op jit(solution)/shard_map/all_to_all | solution.py:33
where the time goes:
time: 421 us; the launch traced here: 417 us
  waiting for transfers between devices  167 us (40%)
  starting transfers between devices  93.6 us (22%)
  blocking collectives  71.5 us (17%)
  local copies, waits for them, and re-layouts  32 us (8%)
  other arithmetic  29.5 us (7%)
  matrix products  16.8 us (4%)
  between operations  7.35 us (2%)
    all_to_all x4, waiting for transfers between devices, sum_at_owner(): lax.all_to_all(blocks, axis, split_axis=0, concat_axis=0, tiled=True)  94.5 us
    all_to_all x5, waiting for transfers between devices, from_everyone(): return lax.all_to_all(copies, axis, split_axis=0, concat_axis=0, tiled=True)  59.4 us
    all_to_all x2, blocking collectives, sum_at_owner(): lax.all_to_all(blocks, axis, split_axis=0, concat_axis=0, tiled=True)  56.9 us
    ppermute x9, starting transfers between devices, shifted(): return lax.ppermute(value, axis, pairs)  50.5 us
    all_to_all x4, starting transfers between devices, sum_at_owner(): lax.all_to_all(blocks, axis, split_axis=0, concat_axis=0, tiled=True)  21.9 us
    all_to_all x5, starting transfers between devices, from_everyone(): return lax.all_to_all(copies, axis, split_axis=0, concat_axis=0, tiled=True)  21.2 us
    all_to_all x1, blocking collectives, from_everyone(): return lax.all_to_all(copies, axis, split_axis=0, concat_axis=0, tiled=True)  14.6 us
    ppermute x9, waiting for transfers between devices, shifted(): return lax.ppermute(value, axis, pairs)  12.7 us
  transfers between devices with their start and end apart: 18, of which 13 were waited for; matrix products, arithmetic and copies ran while one was open for 2% of the time, Pallas kernels for 0%

commit v1 on v0

v1 whole, which is shorter than its diff:
```python
import jax
import jax.numpy as jnp
from jax import lax
from jax.sharding import PartitionSpec as P

HD = 128
NORM_EPS = 1e-05


def shifted(value, axis, steps):
    count = lax.axis_size(axis)
    pairs = [(source, (source + steps) % count) for source in range(count)]
    return lax.ppermute(value, axis, pairs)


def from_everyone(array, axis):
    copies = jnp.broadcast_to(array, (lax.axis_size(axis), *array.shape))
    return lax.all_to_all(copies, axis, split_axis=0, concat_axis=0, tiled=True)


def gather_columns(array, axis):
    blocks = from_everyone(array, axis)
    return jnp.moveaxis(blocks, 0, 1).reshape(array.shape[0], -1)


def layer_norm(x_rows, scale_row):
    widened = x_rows.astype(jnp.float32)
    row_mean = jnp.mean(widened, axis=-1, keepdims=True)
    centered = widened - row_mean
    row_var = jnp.mean(centered * centered, axis=-1, keepdims=True)
    return (centered * lax.rsqrt(row_var + NORM_EPS) * scale_row.astype(jnp.float32)).astype(
        jnp.bfloat16
    )


def context_of(normed, w_in):
    rows = normed.shape[0]
    projected = jnp.dot(
        normed, w_in.reshape(w_in.shape[0], -1), preferred_element_type=jnp.float32
    ).astype(jnp.bfloat16)
    q, k, v = (projected[:, i * HD : (i + 1) * HD] for i in range(3))
    scores = jnp.dot(q, k.T, preferred_element_type=jnp.float32) * HD ** (-0.5)
    causal = jnp.arange(rows)[:, None] >= jnp.arange(rows)[None, :]
    scores = jnp.where(causal, scores, -jnp.inf)
    weights = jnp.exp(scores - jnp.max(scores, axis=-1, keepdims=True))
    probs = (weights / jnp.sum(weights, axis=-1, keepdims=True)).astype(jnp.bfloat16)
    return jnp.dot(probs, v, preferred_element_type=jnp.float32).astype(jnp.bfloat16)


def per_device(pending, admissible, plan, vanished_hop, w_in, w_out, gain):
    last = lax.axis_size("section") - 1
    sections = last + 1
    me = lax.axis_index("section")
    tp = lax.axis_size("tp")
    width = pending.shape[2] // tp
    lost = vanished_hop[0]
    w_in, w_out, gain = w_in[0], w_out[0], gain[0]
    depth = w_out.shape[0]
    by_column = lax.all_to_all(
        jnp.moveaxis(w_out.reshape(depth, tp, width), 1, 0), "tp", 0, 0, tiled=True
    ).reshape(tp * depth, width)
    x_full = jnp.where(me == lost, 0, pending[0]).astype(jnp.bfloat16)
    x_sh = lax.dynamic_slice_in_dim(x_full, lax.axis_index("tp") * width, width, 1)
    entering = [lax.dynamic_index_in_dim(admissible, plan[i], 0, keepdims=False) for i in range(3)]
    late_wrap = (lost == last - 1) | (lost == last - 2)
    ys, fulls = [], []
    for slot in range(5):
        context = gather_columns(context_of(layer_norm(x_full, gain), w_in), "tp")
        y = x_sh.astype(jnp.float32) + jnp.dot(
            context, by_column, preferred_element_type=jnp.float32
        )
        y = y.astype(jnp.bfloat16)
        ys.append(y)
        if slot == 4:
            break
        if slot < 2:
            wrapped = entering[slot]
        elif slot == 2:
            wrapped = jnp.where(late_wrap, entering[2], jnp.where(lost == last, ys[0], y))
        else:
            wrapped = jnp.where(late_wrap, y, entering[2])
        x_sh = shifted(jnp.where(me == last, wrapped, y), "section", 1)
        x_full = gather_columns(x_sh, "tp")
        fulls.append(x_full)
    x4, x5 = fulls[2], fulls[3]
    use5 = jnp.where(me == 0, ~late_wrap, (me > lost) & (me <= lost + 3))
    out = jnp.where(me == lost, 0, jnp.where(use5, x5, x4)).astype(jnp.bfloat16)
    dest = (me + 1) % sections
    early = (dest == (lost + 2) % sections) & (lost <= last - 1)
    late = ((dest == (lost + 3) % sections) & (lost <= last - 1)) | (
        (dest == (lost + 4) % sections) & (lost <= last - 2)
    )
    spare = jnp.where(early, ys[1], jnp.where(late, ys[4], ys[3]))
    return out[None], shifted(spare, "section", 1)[None]


def solution(mesh):
    placed = (
        P("section", None, None),
        P(None, None, "tp"),
        P(),
        P(),
        P("section", None, None, "tp"),
        P("section", "tp", None),
        P("section", None),
    )
    return jax.shard_map(
        per_device,
        mesh=mesh,
        in_specs=placed,
        out_specs=(P("section", None, None), P("section", None, "tp")),
        check_vma=False,
    )
```

time: 421 us -> 259 us (0.62)
  waiting for transfers between devices: 167 us -> 62.7 us
  starting transfers between devices: 93.6 us -> 54.9 us
  other arithmetic: 29.5 us -> 20.6 us
  blocking collectives: 71.5 us -> 65.1 us
  local copies, waits for them, and re-layouts: 32 us -> 25.7 us
    all_to_all x4 -> x1, waiting for transfers between devices: 94.5 us -> 12.4 us  [per_device(): lax.all_to_all(jnp.moveaxis(w_out.reshape(depth, tp, width), 1, 0), 'tp',...]
    all_to_all x2 -> x0, blocking collectives: 56.9 us -> none  [sum_at_owner(): lax.all_to_all(blocks, axis, split_axis=0, concat_axis=0, tiled=True)]
    all_to_all x1 -> x4, blocking collectives: 14.6 us -> 65.1 us  [from_everyone(): return lax.all_to_all(copies, axis, split_axis=0, concat_axis=0, tiled=True)]
    ppermute x9 -> x5, starting transfers between devices: 50.5 us -> 25.6 us  [shifted(): return lax.ppermute(value, axis, pairs)]
    all_to_all x4 -> x1, starting transfers between devices: 21.9 us -> 4.34 us  [per_device(): lax.all_to_all(jnp.moveaxis(w_out.reshape(depth, tp, width), 1, 0), 'tp',...]
    all_to_all x5, waiting for transfers between devices: 59.4 us -> 44.4 us  [from_everyone(): return lax.all_to_all(copies, axis, split_axis=0, concat_axis=0, tiled=True)]
    reduce_sum x10 -> x5, other arithmetic: 8.95 us -> 0.22 us  [context_of(): jnp.sum(weights, axis=-1, keepdims=True)]
    all_to_all x1 -> x4, local copies, waits for them, and re-layouts: 0.65 us -> 9.06 us  [from_everyone(): return lax.all_to_all(copies, axis, split_axis=0, concat_axis=0, tiled=True)]
  transfers between devices with their start and end apart: 18 -> 11, of which waited for: 13 -> 11; matrix products, arithmetic and copies ran while one was open for 2% -> 3% of each run, Pallas kernels for 0% -> 0%
where the time goes in v1:
time: 259 us; the launch traced here: 254 us
  blocking collectives  65.1 us (25%)
  waiting for transfers between devices  62.7 us (24%)
  starting transfers between devices  54.9 us (21%)
  local copies, waits for them, and re-layouts  25.7 us (10%)
  other arithmetic  20.6 us (8%)
  matrix products  17.3 us (7%)
  between operations  7.67 us (3%)
    all_to_all x4, blocking collectives, from_everyone(): return lax.all_to_all(copies, axis, split_axis=0, concat_axis=0, tiled=True)  65.1 us
    all_to_all x5, waiting for transfers between devices, from_everyone(): return lax.all_to_all(copies, axis, split_axis=0, concat_axis=0, tiled=True)  44.4 us
    ppermute x5, starting transfers between devices, shifted(): return lax.ppermute(value, axis, pairs)  25.6 us
    all_to_all x5, starting transfers between devices, from_everyone(): return lax.all_to_all(copies, axis, split_axis=0, concat_axis=0, tiled=True)  25 us
    all_to_all x1, waiting for transfers between devices, per_device(): lax.all_to_all(jnp.moveaxis(w_out.reshape(depth, tp, width), 1, 0), 'tp',...  12.4 us
    all_to_all x4, local copies, waits for them, and re-layouts, from_everyone(): return lax.all_to_all(copies, axis, split_axis=0, concat_axis=0, tiled=True)  9.06 us
    reduce_sum x5, other arithmetic, layer_norm(): row_mean = jnp.mean(widened, axis=-1, keepdims=True)  9.04 us
    dot_general x5, matrix products, per_device(): jnp.dot(context, by_column, preferred_element_type=jnp.float32)  8.73 us
  transfers between devices with their start and end apart: 11, of which 11 were waited for; matrix products, arithmetic and copies ran while one was open for 3% of the time, Pallas kernels for 0%

profile of v1, /device:TPU:1, one launch (start us, length us, event | category | flops | bytes accessed | tf_op | source)
XLA Modules:
  0.0 254.0 jit_solution(6007906302963809636)
XLA Ops:
  4.7 3.2 %copy.15 = bf16[1,4096,3,128]{1,3,2,0:T(8,128)(2,1)S(1)} copy(bf16[1,4096,3,128]{3,1,2,0:T(8,128)(2,1)} %param.11) | data formatting | bytes 6291456 | tf_op args[4]
  7.9 2.3 convolution_convert_fusion.4
  11.5 8.6 %all-to-all-start = ((bf16[16,128,128]{2,1,0:T(8,128)(2,1)}), bf16[16,128,128]{2,1,0:T(8,128)(2,1)}, u32[]{:S(2)}, u32[]{:S(2)}) async-start(bf16[16,128,128]{2,1,0:T(8,128)(2,1)} %broadcast_in_dim.38), calls=%async_computation | async-start | bytes 1048576 | tf_op jit(solution)/shard_map/all_to_all | solution.py:18
  20.1 2.3 copy.16
  22.4 2.3 copy.17
  24.7 5.9 %all-to-all-done = bf16[16,128,128]{2,1,0:T(8,128)(2,1)} async-done(((bf16[16,128,128]{2,1,0:T(8,128)(2,1)}), bf16[16,128,128]{2,1,0:T(8,128)(2,1)}, u32[]{:S(2)}, u32[]{:S(2)}) %all-to-all-start) | async-done | bytes 524320 | tf_op jit(solution)/shard_map/all_to_all | solution.py:18
  30.6 4.3 %all-to-all-start.1 = ((bf16[16,128,256]{2,1,0:T(8,128)(2,1)}), bf16[16,128,256]{2,1,0:T(8,128)(2,1)}, u32[]{:S(2)}, u32[]{:S(2)}) async-start(bf16[16,128,256]{2,1,0:T(8,128)(2,1)} %bitcast.115), calls=%async_computation.1 | async-start | bytes 2097152 | tf_op jit(solution)/shard_map/all_to_all | solution.py:59
  37.6 12.4 %all-to-all-done.1 = bf16[16,128,256]{2,1,0:T(8,128)(2,1)} async-done(((bf16[16,128,256]{2,1,0:T(8,128)(2,1)}), bf16[16,128,256]{2,1,0:T(8,128)(2,1)}, u32[]{:S(2)}, u32[]{:S(2)}) %all-to-all-start.1) | async-done | bytes 1048608 | tf_op jit(solution)/shard_map/all_to_all | solution.py:59
  51.7 2.4 collective-permute-start
  56.9 4.3 %all-to-all-start.2 = ((bf16[16,128,256]{2,1,0:T(8,128)(2,1)}), bf16[16,128,256]{2,1,0:T(8,128)(2,1)}, u32[]{:S(2)}, u32[]{:S(2)}) async-start(bf16[16,128,256]{2,1,0:T(8,128)(2,1)} %broadcast_in_dim.39), calls=%async_computation.2 | async-start | bytes 2097152 | tf_op jit(solution)/shard_map/all_to_all | solution.py:18
  61.3 13.4 %all-to-all-done.2 = bf16[16,128,256]{2,1,0:T(8,128)(2,1)} async-done(((bf16[16,128,256]{2,1,0:T(8,128)(2,1)}), bf16[16,128,256]{2,1,0:T(8,128)(2,1)}, u32[]{:S(2)}, u32[]{:S(2)}) %all-to-all-start.2) | async-done | bytes 1048608 | tf_op jit(solution)/shard_map/all_to_all | solution.py:18
  74.7 2.3 copy.18
  83.7 4.2 %all-to-all-start.3 = ((bf16[16,128,128]{2,1,0:T(8,128)(2,1)}), bf16[16,128,128]{2,1,0:T(8,128)(2,1)}, u32[]{:S(2)}, u32[]{:S(2)}) async-start(bf16[16,128,128]{2,1,0:T(8,128)(2,1)} %broadcast_in_dim.40), calls=%async_computation.3 | async-start | bytes 1048576 | tf_op jit(solution)/shard_map/all_to_all | solution.py:18
  89.9 7.1 %all-to-all-done.3 = bf16[16,128,128]{2,1,0:T(8,128)(2,1)} async-done(((bf16[16,128,128]{2,1,0:T(8,128)(2,1)}), bf16[16,128,128]{2,1,0:T(8,128)(2,1)}, u32[]{:S(2)}, u32[]{:S(2)}) %all-to-all-start.3) | async-done | bytes 524320 | tf_op jit(solution)/shard_map/all_to_all | solution.py:18
  98.7 12.4 %collective-permute-start.1 = (bf16[128,256]{1,0:T(8,128)(2,1)S(1)}, bf16[128,256]{1,0:T(8,128)(2,1)S(1)}, u32[]{:S(2)}, u32[]{:S(2)}) collective-permute-start(bf16[128,256]{1,0:T(8,128)(2,1)S(1)} %get-tuple-element.15), channel_id=1, source_target_pairs={{0,16},{16,32},{32,48},{48,64},{64,80},{80,96},{96,112},{112,0},{1... | collective-permute-start | bytes 196616 | tf_op jit(solution)/shard_map/ppermute | solution.py:13
  112.5 18.6 %all_to_all.50 = bf16[16,128,256]{2,1,0:T(8,128)(2,1)} all-to-all(bf16[16,128,256]{2,1,0:T(8,128)(2,1)S(1)} %broadcast_in_dim.41), channel_id=1, replica_groups=mesh['section'=8,'tp'=16] {'tp'}, dimensions={0} | all-to-all | bytes 2097152 | tf_op jit(solution)/shard_map/all_to_all | solution.py:18
  131.2 2.3 copy.19
  133.4 1.9 convert_reduce_fusion.3
  140.3 4.2 %all-to-all-start.5 = ((bf16[16,128,128]{2,1,0:T(8,128)(2,1)}), bf16[16,128,128]{2,1,0:T(8,128)(2,1)}, u32[]{:S(2)}, u32[]{:S(2)}) async-start(bf16[16,128,128]{2,1,0:T(8,128)(2,1)} %broadcast_in_dim.42), calls=%async_computation.5 | async-start | bytes 1048576 | tf_op jit(solution)/shard_map/all_to_all | solution.py:18
  146.6 9.2 %all-to-all-done.5 = bf16[16,128,128]{2,1,0:T(8,128)(2,1)} async-done(((bf16[16,128,128]{2,1,0:T(8,128)(2,1)}), bf16[16,128,128]{2,1,0:T(8,128)(2,1)}, u32[]{:S(2)}, u32[]{:S(2)}) %all-to-all-start.5) | async-done | bytes 524320 | tf_op jit(solution)/shard_map/all_to_all | solution.py:18
  160.0 17.9 %all_to_all.51 = bf16[16,128,256]{2,1,0:T(8,128)(2,1)} all-to-all(bf16[16,128,256]{2,1,0:T(8,128)(2,1)S(1)} %broadcast_in_dim.43), channel_id=1, replica_groups=mesh['section'=8,'tp'=16] {'tp'}, dimensions={0} | all-to-all | bytes 2097152 | tf_op jit(solution)/shard_map/all_to_all | solution.py:18
  177.9 2.3 copy.20
  180.2 1.9 convert_reduce_fusion.2
  186.2 12.0 %all_to_all.52 = bf16[16,128,128]{2,1,0:T(8,128)(2,1)S(1)} all-to-all(bf16[16,128,128]{2,1,0:T(8,128)(2,1)S(1)} %broadcast_in_dim.44), channel_id=1, replica_groups=mesh['section'=8,'tp'=16] {'tp'}, dimensions={0} | all-to-all | bytes 1048576 | tf_op jit(solution)/shard_map/all_to_all | solution.py:18
  199.8 4.0 %collective-permute-start.3 = (bf16[128,256]{1,0:T(8,128)(2,1)S(1)}, bf16[128,256]{1,0:T(8,128)(2,1)S(1)}, u32[]{:S(2)}, u32[]{:S(2)}) collective-permute-start(bf16[128,256]{1,0:T(8,128)(2,1)S(1)} %get-tuple-element.21), channel_id=1, source_target_pairs={{0,16},{16,32},{32,48},{48,64},{64,80},{80,96},{96,112},{112,0},{1... | collective-permute-start | bytes 196616 | tf_op jit(solution)/shard_map/ppermute | solution.py:13
  205.9 16.5 %all_to_all.53 = bf16[16,128,256]{2,1,0:T(8,128)(2,1)} all-to-all(bf16[16,128,256]{2,1,0:T(8,128)(2,1)S(1)} %broadcast_in_dim.45), channel_id=1, replica_groups=mesh['section'=8,'tp'=16] {'tp'}, dimensions={0} | all-to-all | bytes 2097152 | tf_op jit(solution)/shard_map/all_to_all | solution.py:18
  222.4 2.3 copy.21
  224.7 1.9 convert_reduce_fusion.1
  231.5 3.6 %all-to-all-start.9 = ((bf16[16,128,128]{2,1,0:T(8,128)(2,1)}), bf16[16,128,128]{2,1,0:T(8,128)(2,1)S(1)}, u32[]{:S(2)}, u32[]{:S(2)}) async-start(bf16[16,128,128]{2,1,0:T(8,128)(2,1)} %broadcast_in_dim.46), calls=%async_computation.9 | async-start | bytes 1048576 | tf_op jit(solution)/shard_map/all_to_all | solution.py:18
  235.2 8.9 %all-to-all-done.9 = bf16[16,128,128]{2,1,0:T(8,128)(2,1)S(1)} async-done(((bf16[16,128,128]{2,1,0:T(8,128)(2,1)}), bf16[16,128,128]{2,1,0:T(8,128)(2,1)S(1)}, u32[]{:S(2)}, u32[]{:S(2)}) %all-to-all-start.9) | async-done | bytes 524320 | tf_op jit(solution)/shard_map/all_to_all | solution.py:18
  244.1 2.2 fusion.44
  246.2 5.5 %collective-permute-start.4 = (bf16[128,256]{1,0:T(8,128)(2,1)}, bf16[128,256]{1,0:T(8,128)(2,1)S(1)}, u32[]{:S(2)}, u32[]{:S(2)}) collective-permute-start(bf16[128,256]{1,0:T(8,128)(2,1)} %fusion.44), channel_id=1, source_target_pairs={{0,16},{16,32},{32,48},{48,64},{64,80},{80,96},{96,112},{112,0},{1... | collective-permute-start | bytes 196616 | tf_op jit(solution)/shard_map/ppermute | solution.py:13
  (88 shorter events, 43.8 us)
Async XLA Ops:
  3.6 1.0 copy-start.6
  11.5 19.1 %all-to-all-start = ((bf16[16,128,128]{2,1,0:T(8,128)(2,1)}), bf16[16,128,128]{2,1,0:T(8,128)(2,1)}, u32[]{:S(2)}, u32[]{:S(2)}) async-start(bf16[16,128,128]{2,1,0:T(8,128)(2,1)} %broadcast_in_dim.38), calls=%async_computation | async-start | bytes 1048576 | tf_op jit(solution)/shard_map/all_to_all | solution.py:18
  22.4 12.6 %copy-start.10 = (s32[4]{0:T(128)S(1)}, s32[4]{0:T(128)}, u32[]{:S(2)}) copy-start(s32[4]{0:T(128)} %param.9) | copy-start | bytes 52
  30.6 19.4 %all-to-all-start.1 = ((bf16[16,128,256]{2,1,0:T(8,128)(2,1)}), bf16[16,128,256]{2,1,0:T(8,128)(2,1)}, u32[]{:S(2)}, u32[]{:S(2)}) async-start(bf16[16,128,256]{2,1,0:T(8,128)(2,1)} %bitcast.115), calls=%async_computation.1 | async-start | bytes 2097152 | tf_op jit(solution)/shard_map/all_to_all | solution.py:59
  37.6 23.6 %copy-start.9 = (bf16[1,4096]{1,0:T(2,128)(2,1)S(1)}, bf16[1,4096]{1,0:T(2,128)(2,1)}, u32[]{:S(2)}) copy-start(bf16[1,4096]{1,0:T(2,128)(2,1)} %param.13) | copy-start | bytes 24580
  51.7 4.1 %collective-permute-start = (bf16[128,256]{1,0:T(8,128)(2,1)S(1)}, bf16[128,256]{1,0:T(8,128)(2,1)S(1)}, u32[]{:S(2)}, u32[]{:S(2)}) collective-permute-start(bf16[128,256]{1,0:T(8,128)(2,1)S(1)} %get-tuple-element.11), channel_id=1, source_target_pairs={{0,16},{16,32},{32,48},{48,64},{64,80},{80,96},{96,112},{112,0},{1... | collective-permute-start | bytes 196616 | tf_op jit(solution)/shard_map/ppermute | solution.py:13
  56.9 17.8 %all-to-all-start.2 = ((bf16[16,128,256]{2,1,0:T(8,128)(2,1)}), bf16[16,128,256]{2,1,0:T(8,128)(2,1)}, u32[]{:S(2)}, u32[]{:S(2)}) async-start(bf16[16,128,256]{2,1,0:T(8,128)(2,1)} %broadcast_in_dim.39), calls=%async_computation.2 | async-start | bytes 2097152 | tf_op jit(solution)/shard_map/all_to_all | solution.py:18
  76.9 3.7 %copy-start.4 = (bf16[16,128,256]{1,2,0:T(8,128)(2,1)S(1)}, bf16[16,128,256]{1,2,0:T(8,128)(2,1)}, u32[]{:S(2)}) copy-start(bf16[16,128,256]{1,2,0:T(8,128)(2,1)} %copy.18) | copy-start | bytes 3145732
  83.7 13.2 %all-to-all-start.3 = ((bf16[16,128,128]{2,1,0:T(8,128)(2,1)}), bf16[16,128,128]{2,1,0:T(8,128)(2,1)}, u32[]{:S(2)}, u32[]{:S(2)}) async-start(bf16[16,128,128]{2,1,0:T(8,128)(2,1)} %broadcast_in_dim.40), calls=%async_computation.3 | async-start | bytes 1048576 | tf_op jit(solution)/shard_map/all_to_all | solution.py:18
  98.7 13.8 %collective-permute-start.1 = (bf16[128,256]{1,0:T(8,128)(2,1)S(1)}, bf16[128,256]{1,0:T(8,128)(2,1)S(1)}, u32[]{:S(2)}, u32[]{:S(2)}) collective-permute-start(bf16[128,256]{1,0:T(8,128)(2,1)S(1)} %get-tuple-element.15), channel_id=1, source_target_pairs={{0,16},{16,32},{32,48},{48,64},{64,80},{80,96},{96,112},{112,0},{1... | collective-permute-start | bytes 196616 | tf_op jit(solution)/shard_map/ppermute | solution.py:13
  133.4 3.7 %copy-start.5 = (bf16[16,128,256]{1,2,0:T(8,128)(2,1)S(1)}, bf16[16,128,256]{1,2,0:T(8,128)(2,1)}, u32[]{:S(2)}) copy-start(bf16[16,128,256]{1,2,0:T(8,128)(2,1)} %copy.19) | copy-start | bytes 3145732
  140.3 15.5 %all-to-all-start.5 = ((bf16[16,128,128]{2,1,0:T(8,128)(2,1)}), bf16[16,128,128]{2,1,0:T(8,128)(2,1)}, u32[]{:S(2)}, u32[]{:S(2)}) async-start(bf16[16,128,128]{2,1,0:T(8,128)(2,1)} %broadcast_in_dim.42), calls=%async_computation.5 | async-start | bytes 1048576 | tf_op jit(solution)/shard_map/all_to_all | solution.py:18
  157.4 2.5 collective-permute-start.2
  180.2 3.7 %copy-start = (bf16[16,128,256]{1,2,0:T(8,128)(2,1)S(1)}, bf16[16,128,256]{1,2,0:T(8,128)(2,1)}, u32[]{:S(2)}) copy-start(bf16[16,128,256]{1,2,0:T(8,128)(2,1)} %copy.20) | copy-start | bytes 3145732
  199.8 5.4 %collective-permute-start.3 = (bf16[128,256]{1,0:T(8,128)(2,1)S(1)}, bf16[128,256]{1,0:T(8,128)(2,1)S(1)}, u32[]{:S(2)}, u32[]{:S(2)}) collective-permute-start(bf16[128,256]{1,0:T(8,128)(2,1)S(1)} %get-tuple-element.21), channel_id=1, source_target_pairs={{0,16},{16,32},{32,48},{48,64},{64,80},{80,96},{96,112},{112,0},{1... | collective-permute-start | bytes 196616 | tf_op jit(solution)/shard_map/ppermute | solution.py:13
  205.1 0.6 copy-start.7
  224.7 3.7 %copy-start.2 = (bf16[16,128,256]{1,2,0:T(8,128)(2,1)S(1)}, bf16[16,128,256]{1,2,0:T(8,128)(2,1)}, u32[]{:S(2)}) copy-start(bf16[16,128,256]{1,2,0:T(8,128)(2,1)} %copy.21) | copy-start | bytes 3145732
  230.2 13.9 %copy-start.8 = (bf16[128,256]{1,0:T(8,128)(2,1)S(1)}, bf16[128,256]{1,0:T(8,128)(2,1)}, u32[]{:S(2)}) copy-start(bf16[128,256]{1,0:T(8,128)(2,1)} %copy-done.7) | copy-start | bytes 196612
  230.4 21.4 %copy-start.1 = (bf16[16,128,256]{1,2,0:T(8,128)(2,1)S(1)}, bf16[16,128,256]{1,2,0:T(8,128)(2,1)}, u32[]{:S(2)}) copy-start(bf16[16,128,256]{1,2,0:T(8,128)(2,1)} %copy.20) | copy-start | bytes 3145732
  230.4 21.4 %copy-start.3 = (bf16[16,128,256]{1,2,0:T(8,128)(2,1)S(1)}, bf16[16,128,256]{1,2,0:T(8,128)(2,1)}, u32[]{:S(2)}) copy-start(bf16[16,128,256]{1,2,0:T(8,128)(2,1)} %copy.21) | copy-start | bytes 3145732
  231.5 12.5 %all-to-all-start.9 = ((bf16[16,128,128]{2,1,0:T(8,128)(2,1)}), bf16[16,128,128]{2,1,0:T(8,128)(2,1)S(1)}, u32[]{:S(2)}, u32[]{:S(2)}) async-start(bf16[16,128,128]{2,1,0:T(8,128)(2,1)} %broadcast_in_dim.46), calls=%async_computation.9 | async-start | bytes 1048576 | tf_op jit(solution)/shard_map/all_to_all | solution.py:18
  246.2 7.2 %collective-permute-start.4 = (bf16[128,256]{1,0:T(8,128)(2,1)}, bf16[128,256]{1,0:T(8,128)(2,1)S(1)}, u32[]{:S(2)}, u32[]{:S(2)}) collective-permute-start(bf16[128,256]{1,0:T(8,128)(2,1)} %fusion.44), channel_id=1, source_target_pairs={{0,16},{16,32},{32,48},{48,64},{64,80},{80,96},{96,112},{112,0},{1... | collective-permute-start | bytes 196616 | tf_op jit(solution)/shard_map/ppermute | solution.py:13

commit v2 on v1

v2 whole, which is shorter than its diff:
```python
import functools

import jax
import jax.numpy as jnp
from jax import lax
from jax.experimental import pallas as pl
from jax.experimental.pallas import tpu as pltpu
from jax.sharding import PartitionSpec as P

HD = 128
LANES = 128
SLOTS = 5
CHUNKS = 2
NORM_EPS = 1e-05
MESH = pl.DeviceIdType.MESH


def arrive(ref, sem):
    pltpu.make_async_copy(ref, ref, sem).wait()


def kernel(
    side,
    pending,
    admissible,
    plan,
    vanished,
    w_in_hbm,
    w_out_hbm,
    gain,
    out_ref,
    standby_ref,
    x_raw,
    w_in,
    w_out,
    x,
    ctx,
    y_real,
    y_send,
    normed,
    keys,
    values,
    spare,
    load_sem,
    wo_sem,
    ctx_sem,
    one_sem,
    two_sem,
    end_sem,
):
    sections = lax.axis_size("section")
    section = lax.axis_index("section")
    tp = lax.axis_index("tp")
    count = side * side
    z, y = tp // side, tp % side
    following = (section + 1) % sections
    rows, width = pending.shape[0], pending.shape[1]
    part = rows // CHUNKS
    cols = width // count
    halves = cols // LANES
    lost = vanished[0]
    final = sections - 1
    late_wrap = (lost == final - 1) | (lost == final - 2)

    def send(src, dst, sems, where):
        copy = pltpu.make_async_remote_copy(
            src_ref=src,
            dst_ref=dst,
            send_sem=sems.at[0],
            recv_sem=sems.at[1],
            device_id=where,
            device_id_type=MESH,
        )
        copy.start()

    def others(dz, dy):
        return ((z + dz) % side) * side + (y + dy) % side

    steps = [(a, b) for a in range(side) for b in range(side) if a or b]

    load_x = pltpu.make_async_copy(pending, x_raw, load_sem.at[0])
    load_x.start()
    loads = [
        pltpu.make_async_copy(
            w_in_hbm.at[j], w_in.at[:, pl.ds(j * HD, HD)], load_sem.at[1 + j]
        )
        for j in range(3)
    ]
    for load in loads:
        load.start()
    own = pltpu.make_async_copy(
        w_out_hbm.at[:, pl.ds(pl.multiple_of(tp * cols, LANES), cols)], w_out.at[tp], load_sem.at[4]
    )
    own.start()
    for dz, dy in steps:
        peer = others(dz, dy)
        send(
            w_out_hbm.at[:, pl.ds(pl.multiple_of(peer * cols, LANES), cols)],
            w_out.at[tp],
            wo_sem,
            (section, peer),
        )
    load_x.wait()
    for c in range(count):
        for h in range(halves):
            for r in range(CHUNKS):
                block = x_raw[r * part : (r + 1) * part, c * cols + h * LANES : c * cols + (h + 1) * LANES]
                x[0, r, h, c // side, c % side] = jnp.where(section == lost, jnp.zeros_like(block), block)
    for load in loads:
        load.wait()

    def heads(k, r):
        def blocks():
            for c in range(count):
                for h in range(halves):
                    yield c * cols + h * LANES, x[k, r, h, c // side, c % side].astype(jnp.float32)

        total = jnp.zeros((part, LANES), jnp.float32)
        for _, block in blocks():
            total = total + block
        mean = jnp.sum(total, axis=-1, keepdims=True) * (1.0 / width)
        total = jnp.zeros((part, LANES), jnp.float32)
        for _, block in blocks():
            block = block - mean
            total = total + block * block
        scale = lax.rsqrt(jnp.sum(total, axis=-1, keepdims=True) * (1.0 / width) + NORM_EPS)
        for at, block in blocks():
            g = gain[:, at : at + LANES].astype(jnp.float32)
            normed[:, at : at + LANES] = ((block - mean) * scale * g).astype(jnp.bfloat16)
        projected = jnp.dot(normed[...], w_in[...], preferred_element_type=jnp.float32).astype(
            jnp.bfloat16
        )
        keys[r * part : (r + 1) * part, :] = projected[:, HD : 2 * HD]
        values[r * part : (r + 1) * part, :] = projected[:, 2 * HD :]
        seen = (r + 1) * part
        scores = lax.dot_general(
            projected[:, :HD],
            keys[:seen, :],
            (((1,), (1,)), ((), ())),
            preferred_element_type=jnp.float32,
        ) * HD ** (-0.5)
        row = lax.broadcasted_iota(jnp.int32, (part, seen), 0) + r * part
        col = lax.broadcasted_iota(jnp.int32, (part, seen), 1)
        scores = jnp.where(row >= col, scores, -jnp.inf)
        weights = jnp.exp(scores - jnp.max(scores, axis=-1, keepdims=True))
        probs = (weights / jnp.sum(weights, axis=-1, keepdims=True)).astype(jnp.bfloat16)
        mixed = jnp.dot(probs, values[:seen, :], preferred_element_type=jnp.float32)
        ctx[k, r, tp] = mixed.astype(jnp.bfloat16)
        for dz, dy in steps:
            send(ctx.at[k, r, tp], ctx.at[k, r, tp], ctx_sem.at[k, r], (section, others(dz, dy)))

    def mix(k, r):
        arrive(ctx.at[k, r, pl.ds(0, count - 1)], ctx_sem.at[k, r, 1])
        context = jnp.concatenate([ctx[k, r, i] for i in range(count)], axis=1)
        weights = w_out[...].reshape(count * HD, cols)
        branch = jnp.dot(context, weights, preferred_element_type=jnp.float32)
        mine = jnp.concatenate([x[k, r, h, z, y] for h in range(halves)], axis=1)
        result = (mine.astype(jnp.float32) + branch).astype(jnp.bfloat16)
        y_real[k, r] = result

        @pl.when(k < SLOTS - 1)
        def _():
            entering = admissible[plan[jnp.minimum(k, 2)], r * part : (r + 1) * part, :]
            enters = (k < 2) | ((k == 2) & late_wrap) | ((k == 3) & jnp.logical_not(late_wrap))
            held = jnp.where((k == 2) & (lost == final), y_real[0, r], result)
            wrapped = jnp.where(enters, entering, held)
            sent = jnp.where(section == final, wrapped, result)
            for h in range(halves):
                y_send[k, r, h] = sent[:, h * LANES : (h + 1) * LANES]
                for step in range(side):
                    peer = others(step, 0) if h == 0 else others(0, step)
                    send(
                        y_send.at[k, r, h],
                        x.at[k + 1, r, h, z, y],
                        one_sem.at[k, r, h],
                        (following, peer),
                    )

    def line(k, r, h):
        return x.at[k + 1, r, h, :, y] if h == 0 else x.at[k + 1, r, h, z]

    def forward(k, r):
        for h in range(halves):
            arrive(x.at[k + 1, r, h, 0], one_sem.at[k, r, h, 1])
            for step in range(1, side):
                peer = others(0, step) if h == 0 else others(step, 0)
                send(line(k, r, h), line(k, r, h), two_sem.at[k, r, h], (section, peer))

    def gathered(k, r):
        for h in range(halves):
            arrive(x.at[k + 1, r, h, pl.ds(0, side - 1)], two_sem.at[k, r, h, 1])

    def slot(k, carry):
        for r in range(CHUNKS):

            @pl.when(k > 0)
            def _():
                gathered(k - 1, r)

            heads(k, r)

        @pl.when(k == 0)
        def _():
            own.wait()
            arrive(w_out.at[pl.ds(0, count - 1)], wo_sem.at[1])

        @pl.when(k == SLOTS - 1)
        def _():
            behind = (section > lost) & (section <= lost + 3)
            newest = jnp.where(section == 0, jnp.logical_not(late_wrap), behind)
            for c in range(count):
                for h in range(halves):
                    for r in range(CHUNKS):
                        at = (r, h, c // side, c % side)
                        block = jnp.where(newest, x[SLOTS - 1, *at], x[SLOTS - 2, *at])
                        block = jnp.where(section == lost, jnp.zeros_like(block), block)
                        start = c * cols + h * LANES
                        out_ref[r * part : (r + 1) * part, start : start + LANES] = block

        for r in range(CHUNKS):
            mix(k, r)

        @pl.when(k < SLOTS - 1)
        def _():
            for r in range(CHUNKS):
                forward(k, r)

        return carry

    lax.fori_loop(0, SLOTS, slot, 0)

    target = (section + 1) % sections
    early = (target == (lost + 2) % sections) & (lost <= final - 1)
    late = ((target == (lost + 3) % sections) & (lost <= final - 1)) | (
        (target == (lost + 4) % sections) & (lost <= final - 2)
    )
    for r in range(CHUNKS):
        chosen = jnp.where(early, y_real[1, r], jnp.where(late, y_real[4, r], y_real[3, r]))
        spare[r] = chosen
        send(spare.at[r], standby_ref.at[pl.ds(r * part, part)], end_sem.at[r], (following, tp))

    arrive(w_out.at[pl.ds(0, count - 1)], wo_sem.at[0])

    def drain(k, carry):
        for r in range(CHUNKS):
            arrive(ctx.at[k, r, pl.ds(0, count - 1)], ctx_sem.at[k, r, 0])

            @pl.when(k < SLOTS - 1)
            def _():
                for h in range(halves):
                    arrive(x.at[k, r, h, 0], one_sem.at[k, r, h, 0])
                    arrive(x.at[k, r, h, pl.ds(0, side - 1)], two_sem.at[k, r, h, 0])

        return carry

    lax.fori_loop(0, SLOTS, drain, 0)
    for r in range(CHUNKS):
        arrive(spare.at[r], end_sem.at[r, 0])
        arrive(spare.at[r], end_sem.at[r, 1])


def per_device(pending, admissible, plan, vanished_hop, w_in, w_out, gain):
    count = lax.axis_size("tp")
    side = int(round(count**0.5))
    rows, width = pending.shape[1:]
    cols = width // count
    part = rows // CHUNKS
    halves = cols // LANES
    vmem = pl.BlockSpec(memory_space=pltpu.VMEM)
    smem = pl.BlockSpec(memory_space=pltpu.SMEM)
    anywhere = pl.BlockSpec(memory_space=pl.ANY)
    bf16 = jnp.bfloat16
    dma = pltpu.SemaphoreType.DMA
    out, standby = pl.pallas_call(
        functools.partial(kernel, side),
        out_shape=(
            jax.ShapeDtypeStruct((rows, width), bf16),
            jax.ShapeDtypeStruct((rows, cols), bf16),
        ),
        in_specs=[anywhere, vmem, smem, smem, anywhere, anywhere, vmem],
        out_specs=(vmem, anywhere),
        scratch_shapes=[
            pltpu.VMEM((rows, width), bf16),
            pltpu.VMEM((width, 3 * HD), bf16),
            pltpu.VMEM((count, HD, cols), bf16),
            pltpu.VMEM((SLOTS, CHUNKS, halves, side, side, part, LANES), bf16),
            pltpu.VMEM((SLOTS, CHUNKS, count, part, HD), bf16),
            pltpu.VMEM((SLOTS, CHUNKS, part, cols), bf16),
            pltpu.VMEM((SLOTS - 1, CHUNKS, halves, part, LANES), bf16),
            pltpu.VMEM((part, width), bf16),
            pltpu.VMEM((rows, HD), bf16),
            pltpu.VMEM((rows, HD), bf16),
            pltpu.VMEM((CHUNKS, part, cols), bf16),
            dma((5,)),
            dma((2,)),
            dma((SLOTS, CHUNKS, 2)),
            dma((SLOTS - 1, CHUNKS, halves, 2)),
            dma((SLOTS - 1, CHUNKS, halves, 2)),
            dma((CHUNKS, 2)),
        ],
        compiler_params=pltpu.CompilerParams(
            has_side_effects=True, vmem_limit_bytes=48 * 1024 * 1024
        ),
        name="relay",
    )(
        pending[0],
        admissible,
        plan,
        vanished_hop,
        jnp.moveaxis(w_in[0], 1, 0),
        w_out[0],
        gain,
    )
    return out[None], standby[None]


def solution(mesh):
    placed = (
        P("section", None, None),
        P(None, None, "tp"),
        P(),
        P(),
        P("section", None, None, "tp"),
        P("section", "tp", None),
        P("section", None),
    )
    return jax.shard_map(
        per_device,
        mesh=mesh,
        in_specs=placed,
        out_specs=(P("section", None, None), P("section", None, "tp")),
        check_vma=False,
    )
```

time: 259 us -> 120 us (0.46); the launches traced: 254 us -> 120 us
  Pallas kernels: 0 us -> 112 us
  blocking collectives: 65.1 us -> 0 us
  waiting for transfers between devices: 62.7 us -> 0 us
  starting transfers between devices: 54.9 us -> 0 us
  other arithmetic: 20.6 us -> 0 us
  local copies, waits for them, and re-layouts: 25.7 us -> 6.36 us
  matrix products: 17.3 us -> 0 us
  between operations: 7.67 us -> 1.3 us
    pallas_call x0 -> x1, Pallas kernels: none -> 112 us  [per_device(): pl.pallas_call(functools.partial(kernel, side), out_shape=(jax.ShapeDtype...]
    all_to_all x4 -> x0, blocking collectives: 65.1 us -> none  [from_everyone(): return lax.all_to_all(copies, axis, split_axis=0, concat_axis=0, tiled=True)]
    all_to_all x6 -> x0, waiting for transfers between devices: 56.9 us -> none  [the longest x5 44.4 us: from_everyone(): return lax.all_to_all(copies, axis, split_axis=0, concat_axis=0, tiled=True)]
    all_to_all x6 -> x0, starting transfers between devices: 29.4 us -> none  [the longest x5 25 us: from_everyone(): return lax.all_to_all(copies, axis, split_axis=0, concat_axis=0, tiled=True)]
    ppermute x5 -> x0, starting transfers between devices: 25.6 us -> none  [shifted(): return lax.ppermute(value, axis, pairs)]
    dot_general x20 -> x0, matrix products: 17.3 us -> none  [the longest x5 8.73 us: per_device(): jnp.dot(context, by_column, preferred_element_type=jnp.float32)]
    reduce_sum x15 -> x0, other arithmetic: 16.8 us -> none  [the longest x5 9.04 us: layer_norm(): row_mean = jnp.mean(widened, axis=-1, keepdims=True)]
    all_to_all x4 -> x0, local copies, waits for them, and re-layouts: 9.06 us -> none  [from_everyone(): return lax.all_to_all(copies, axis, split_axis=0, concat_axis=0, tiled=True)]
  transfers between devices with their start and end apart: 11 -> 0, of which waited for: 11 -> 0; matrix products, arithmetic and copies ran while one was open for 3% -> 0% of each run, Pallas kernels for 0% -> 0%
where the time goes in v2:
time: 120 us
  Pallas kernels  112 us (93%)
  local copies, waits for them, and re-layouts  6.36 us (5%)
  between operations  1.3 us (1%)
    pallas_call x1, Pallas kernels, per_device(): pl.pallas_call(functools.partial(kernel, side), out_shape=(jax.ShapeDtype...  112 us
    unnamed x12, local copies, waits for them, and re-layouts  6.36 us

profile of v2, /device:TPU:1, one launch (start us, length us, event | category | flops | bytes accessed | tf_op | source)
XLA Modules:
  0.0 120.1 jit_solution(6122276183323842418)
XLA Ops:
  1.3 0.0 copy-start
  1.3 1.2 %copy-done = bf16[1,128,4096]{2,1,0:T(8,128)(2,1)S(1)} copy-done((bf16[1,128,4096]{2,1,0:T(8,128)(2,1)S(1)}, bf16[1,128,4096]{2,1,0:T(8,128)(2,1)}, u32[]{:S(2)}) %copy-start) | copy-done | bytes 1048600
  2.5 0.0 copy-start.1
  2.5 1.2 %copy-done.1 = bf16[1,128,4096]{2,1,0:T(8,128)(2,1)S(1)} copy-done((bf16[1,128,4096]{2,1,0:T(8,128)(2,1)S(1)}, bf16[1,128,4096]{2,1,0:T(8,128)(2,1)}, u32[]{:S(2)}) %copy-start.1) | copy-done | bytes 1048600
  3.7 0.0 copy-start.2
  3.7 0.9 copy-done.2
  4.7 0.0 copy-start.3
  4.7 0.7 copy-done.3
  5.4 0.0 copy-start.4
  5.4 0.7 copy-done.4
  6.1 112.5 %relay.1 = (bf16[128,4096]{1,0:T(8,128)(2,1)S(1)}, bf16[128,256]{1,0:T(8,128)(2,1)S(1)}) custom-call(bf16[128,4096]{1,0:T(8,128)(2,1)S(1)} %bitcast.8, bf16[4,128,256]{2,1,0:T(8,128)(2,1)S(1)} %copy-done.2, s32[4]{0:T(128)S(1)} %copy-done.4, s32[1]{0:T(128)S(6)} %copy.11.vanished, bf16[3,4096,128]{2,1,0:T(8,128)(2,1)} %bitcast.11, ...), custom_call_target="tpu_custom_call" | custom-call | tf_op jit(solution)/shard_map/relay/pallas_call | solution.py:274
  118.5 1.0 copy.12
  119.5 0.6 copy.13
Async XLA Ops:
  1.3 1.2 %copy-start = (bf16[1,128,4096]{2,1,0:T(8,128)(2,1)S(1)}, bf16[1,128,4096]{2,1,0:T(8,128)(2,1)}, u32[]{:S(2)}) copy-start(bf16[1,128,4096]{2,1,0:T(8,128)(2,1)} %param.7) | copy-start | bytes 3145732
  2.5 1.2 %copy-start.1 = (bf16[1,128,4096]{2,1,0:T(8,128)(2,1)S(1)}, bf16[1,128,4096]{2,1,0:T(8,128)(2,1)}, u32[]{:S(2)}) copy-start(bf16[1,128,4096]{2,1,0:T(8,128)(2,1)} %param.12) | copy-start | bytes 3145732
  3.7 0.9 copy-start.2
  4.7 0.7 copy-start.3
  5.4 0.7 copy-start.4

commit v3 on v2

--- a/solution.py
+++ b/solution.py
@@ -22,12 +22,12 @@
 def kernel(
     side,
     pending,
-    admissible,
-    plan,
+    admissible_hbm,
+    plan_hbm,
     vanished,
     w_in_hbm,
     w_out_hbm,
-    gain,
+    gain_hbm,
     out_ref,
     standby_ref,
     x_raw,
@@ -41,6 +41,9 @@
     keys,
     values,
     spare,
+    admissible,
+    gain,
+    plan,
     load_sem,
     wo_sem,
     ctx_sem,
@@ -54,13 +57,11 @@
     count = side * side
     z, y = tp // side, tp % side
     following = (section + 1) % sections
+    final = sections - 1
     rows, width = pending.shape[0], pending.shape[1]
     part = rows // CHUNKS
     cols = width // count
     halves = cols // LANES
-    lost = vanished[0]
-    final = sections - 1
-    late_wrap = (lost == final - 1) | (lost == final - 2)
 
     def send(src, dst, sems, where):
         copy = pltpu.make_async_remote_copy(
@@ -76,7 +77,26 @@
     def others(dz, dy):
         return ((z + dz) % side) * side + (y + dy) % side
 
-    steps = [(a, b) for a in range(side) for b in range(side) if a or b]
+    steps = sorted(
+        ((a, b) for a in range(side) for b in range(side) if a or b),
+        key=lambda s: -sum(min(d, side - d) for d in s),
+    )
+
+    barrier = pltpu.get_barrier_semaphore()
+    before = (section + final) % sections
+    senders = [(section, others(dz, dy)) for dz, dy in steps]
+    senders += [(before, others(d, 0)) for d in range(side)]
+    senders += [(before, others(0, d)) for d in range(1, side)]
+    for sender in senders:
+        pl.semaphore_signal(barrier, inc=1, device_id=sender, device_id_type=MESH)
+    smalls = [
+        pltpu.make_async_copy(src, dst, load_sem.at[5 + i])
+        for i, (src, dst) in enumerate(
+            ((plan_hbm, plan), (gain_hbm, gain), (admissible_hbm, admissible))
+        )
+    ]
+    for load in smalls:
+        load.start()
 
     load_x = pltpu.make_async_copy(pending, x_raw, load_sem.at[0])
     load_x.start()
@@ -92,6 +112,7 @@
         w_out_hbm.at[:, pl.ds(pl.multiple_of(tp * cols, LANES), cols)], w_out.at[tp], load_sem.at[4]
     )
     own.start()
+    pl.semaphore_wait(barrier, len(senders))
     for dz, dy in steps:
         peer = others(dz, dy)
         send(
@@ -100,6 +121,10 @@
             wo_sem,
             (section, peer),
         )
+    for load in smalls:
+        load.wait()
+    lost = vanished[0]
+    late_wrap = (lost == final - 1) | (lost == final - 2)
     load_x.wait()
     for c in range(count):
         for h in range(halves):
@@ -259,6 +284,10 @@
         arrive(spare.at[r], end_sem.at[r, 1])
 
 
+def in_hbm(array):
+    return pltpu.with_memory_space_constraint(array, pltpu.HBM)
+
+
 def per_device(pending, admissible, plan, vanished_hop, w_in, w_out, gain):
     count = lax.axis_size("tp")
     side = int(round(count**0.5))
@@ -268,7 +297,7 @@
     halves = cols // LANES
     vmem = pl.BlockSpec(memory_space=pltpu.VMEM)
     smem = pl.BlockSpec(memory_space=pltpu.SMEM)
-    anywhere = pl.BlockSpec(memory_space=pl.ANY)
+    hbm = pl.BlockSpec(memory_space=pltpu.HBM)
     bf16 = jnp.bfloat16
     dma = pltpu.SemaphoreType.DMA
     out, standby = pl.pallas_call(
@@ -277,8 +306,8 @@
             jax.ShapeDtypeStruct((rows, width), bf16),
             jax.ShapeDtypeStruct((rows, cols), bf16),
         ),
-        in_specs=[anywhere, vmem, smem, smem, anywhere, anywhere, vmem],
-        out_specs=(vmem, anywhere),
+        in_specs=[hbm] * 3 + [smem] + [hbm] * 3,
+        out_specs=(vmem, vmem),
         scratch_shapes=[
             pltpu.VMEM((rows, width), bf16),
             pltpu.VMEM((width, 3 * HD), bf16),
@@ -291,7 +320,10 @@
             pltpu.VMEM((rows, HD), bf16),
             pltpu.VMEM((rows, HD), bf16),
             pltpu.VMEM((CHUNKS, part, cols), bf16),
-            dma((5,)),
+            pltpu.VMEM(admissible.shape, bf16),
+            pltpu.VMEM(gain.shape, bf16),
+            pltpu.SMEM(plan.shape, jnp.int32),
+            dma((8,)),
             dma((2,)),
             dma((SLOTS, CHUNKS, 2)),
             dma((SLOTS - 1, CHUNKS, halves, 2)),
@@ -299,17 +331,17 @@
             dma((CHUNKS, 2)),
         ],
         compiler_params=pltpu.CompilerParams(
-            has_side_effects=True, vmem_limit_bytes=48 * 1024 * 1024
+            has_side_effects=True, vmem_limit_bytes=48 * 1024 * 1024, collective_id=0
         ),
         name="relay",
     )(
-        pending[0],
-        admissible,
-        plan,
+        in_hbm(pending[0]),
+        in_hbm(admissible),
+        in_hbm(plan),
         vanished_hop,
-        jnp.moveaxis(w_in[0], 1, 0),
-        w_out[0],
-        gain,
+        in_hbm(jnp.moveaxis(w_in[0], 1, 0)),
+        in_hbm(w_out[0]),
+        in_hbm(gain),
     )
     return out[None], standby[None]
 

time: 120 us -> 106 us (0.88)
  Pallas kernels: 112 us -> 103 us
  local copies, waits for them, and re-layouts: 6.36 us -> 1.6 us
    pallas_call x1, Pallas kernels: 112 us -> 103 us  [per_device(): pl.pallas_call(functools.partial(kernel, side), out_shape=(jax.ShapeDtype...]
    unnamed x12 -> x2, local copies, waits for them, and re-layouts: 6.36 us -> 1.6 us
where the time goes in v3:
time: 106 us
  Pallas kernels  103 us (97%)
  local copies, waits for them, and re-layouts  1.6 us (2%)
  between operations  1.29 us (1%)
    pallas_call x1, Pallas kernels, per_device(): pl.pallas_call(functools.partial(kernel, side), out_shape=(jax.ShapeDtype...  103 us

profile of v3, /device:TPU:1, one launch (start us, length us, event | category | flops | bytes accessed | tf_op | source)
XLA Modules:
  0.0 106.1 jit_solution(3121449800681079780)
XLA Ops:
  1.3 103.2 %relay.1 = (bf16[128,4096]{1,0:T(8,128)(2,1)S(1)}, bf16[128,256]{1,0:T(8,128)(2,1)S(1)}) custom-call(bf16[128,4096]{1,0:T(8,128)(2,1)} %bitcast.10, bf16[4,128,256]{2,1,0:T(8,128)(2,1)} %admissible_hbm.1, s32[4]{0:T(128)} %plan_hbm.1, s32[1]{0:T(128)S(6)} %copy.11.vanished, bf16[3,4096,128]{2,1,0:T(8,128)(2,1)} %bitcast.9, bf16[128,4096]{1,0:T(8,128)(2,1)} %bitcast.11, ...), custom_call_target="tpu_custom_call" | custom-call | tf_op jit(solution)/shard_map/relay/pallas_call | solution.py:303
  104.5 1.0 copy.12
  105.5 0.6 copy.13

commit v4 on v3

--- a/solution.py
+++ b/solution.py
@@ -10,7 +10,7 @@
 HD = 128
 LANES = 128
 SLOTS = 5
-CHUNKS = 2
+CHUNKS = 4
 NORM_EPS = 1e-05
 MESH = pl.DeviceIdType.MESH
 
@@ -215,6 +215,13 @@
         for h in range(halves):
             arrive(x.at[k + 1, r, h, pl.ds(0, side - 1)], two_sem.at[k, r, h, 1])
 
+    def left(k):
+        for r in range(CHUNKS):
+            arrive(ctx.at[k, r, pl.ds(0, count - 1)], ctx_sem.at[k, r, 0])
+            for h in range(halves):
+                arrive(x.at[k, r, h, 0], one_sem.at[k, r, h, 0])
+                arrive(x.at[k, r, h, pl.ds(0, side - 1)], two_sem.at[k, r, h, 0])
+
     def slot(k, carry):
         for r in range(CHUNKS):
 
@@ -231,6 +238,7 @@
 
         @pl.when(k == SLOTS - 1)
         def _():
+            arrive(w_out.at[pl.ds(0, count - 1)], wo_sem.at[0])
             behind = (section > lost) & (section <= lost + 3)
             newest = jnp.where(section == 0, jnp.logical_not(late_wrap), behind)
             for c in range(count):
@@ -242,12 +250,22 @@
                         start = c * cols + h * LANES
                         out_ref[r * part : (r + 1) * part, start : start + LANES] = block
 
-        for r in range(CHUNKS):
+        @pl.when(k > 0)
+        def _():
+            left(k - 1)
+
+        for r in range(CHUNKS - 1):
             mix(k, r)
 
         @pl.when(k < SLOTS - 1)
         def _():
-            for r in range(CHUNKS):
+            forward(k, 0)
+
+        mix(k, CHUNKS - 1)
+
+        @pl.when(k < SLOTS - 1)
+        def _():
+            for r in range(1, CHUNKS):
                 forward(k, r)
 
         return carry
@@ -264,21 +282,8 @@
         spare[r] = chosen
         send(spare.at[r], standby_ref.at[pl.ds(r * part, part)], end_sem.at[r], (following, tp))
 
-    arrive(w_out.at[pl.ds(0, count - 1)], wo_sem.at[0])
-
-    def drain(k, carry):
-        for r in range(CHUNKS):
-            arrive(ctx.at[k, r, pl.ds(0, count - 1)], ctx_sem.at[k, r, 0])
-
-            @pl.when(k < SLOTS - 1)
-            def _():
-                for h in range(halves):
-                    arrive(x.at[k, r, h, 0], one_sem.at[k, r, h, 0])
-                    arrive(x.at[k, r, h, pl.ds(0, side - 1)], two_sem.at[k, r, h, 0])
-
-        return carry
-
-    lax.fori_loop(0, SLOTS, drain, 0)
+    for r in range(CHUNKS):
+        arrive(ctx.at[SLOTS - 1, r, pl.ds(0, count - 1)], ctx_sem.at[SLOTS - 1, r, 0])
     for r in range(CHUNKS):
         arrive(spare.at[r], end_sem.at[r, 0])
         arrive(spare.at[r], end_sem.at[r, 1])

time: 106 us -> 97.7 us (0.922)
  Pallas kernels: 103 us -> 94.7 us
    pallas_call x1, Pallas kernels: 103 us -> 94.7 us  [per_device(): pl.pallas_call(functools.partial(kernel, side), out_shape=(jax.ShapeDtype...]
where the time goes in v4:
time: 97.7 us; the launch traced here: 97.5 us
  Pallas kernels  94.7 us (97%)
  local copies, waits for them, and re-layouts  1.6 us (2%)
  between operations  1.29 us (1%)
    pallas_call x1, Pallas kernels, per_device(): pl.pallas_call(functools.partial(kernel, side), out_shape=(jax.ShapeDtype...  94.7 us

profile of v4, /device:TPU:1, one launch (start us, length us, event | category | flops | bytes accessed | tf_op | source)
XLA Modules:
  0.0 97.5 jit_solution(9526970781097153833)
XLA Ops:
  1.3 94.7 %relay.1 = (bf16[128,4096]{1,0:T(8,128)(2,1)S(1)}, bf16[128,256]{1,0:T(8,128)(2,1)S(1)}) custom-call(bf16[128,4096]{1,0:T(8,128)(2,1)} %bitcast.10, bf16[4,128,256]{2,1,0:T(8,128)(2,1)} %admissible_hbm.1, s32[4]{0:T(128)} %plan_hbm.1, s32[1]{0:T(128)S(6)} %copy.11.vanished, bf16[3,4096,128]{2,1,0:T(8,128)(2,1)} %bitcast.9, bf16[128,4096]{1,0:T(8,128)(2,1)} %bitcast.11, ...), custom_call_target="tpu_custom_call" | custom-call | tf_op jit(solution)/shard_map/relay/pallas_call | solution.py:308
  95.9 1.0 copy.12
  96.9 0.6 copy.13

commit v5 on v4

v5 whole, which is shorter than its diff:
```python
import functools

import jax
import jax.numpy as jnp
from jax import lax
from jax.experimental import pallas as pl
from jax.experimental.pallas import tpu as pltpu
from jax.sharding import PartitionSpec as P

HD = 128
LANES = 128
SLOTS = 5
CHUNKS = 4
NORM_EPS = 1e-05
MESH = pl.DeviceIdType.MESH


def arrive(ref, sem):
    pltpu.make_async_copy(ref, ref, sem).wait()


def kernel(
    side,
    pending,
    admissible_hbm,
    plan_hbm,
    vanished,
    w_in_hbm,
    w_out_hbm,
    gain_hbm,
    out_ref,
    standby_ref,
    x_raw,
    w_in,
    w_line,
    x,
    ctx,
    kept,
    sent,
    got,
    total,
    normed,
    keys,
    values,
    spare,
    spare_got,
    admissible,
    gain,
    plan,
    load_sem,
    wo_sem,
    ctx_sem,
    part_sem,
    sum_sem,
    end_sem,
):
    sections = lax.axis_size("section")
    section = lax.axis_index("section")
    tp = lax.axis_index("tp")
    count = side * side
    z, y = tp // side, tp % side
    place = (z, y)
    final = sections - 1
    following = (section + 1) % sections
    before = (section + final) % sections
    rows, width = pending.shape[0], pending.shape[1]
    part = rows // CHUNKS
    cols = width // count
    halves = cols // LANES

    def send(src, dst, sems, where):
        copy = pltpu.make_async_remote_copy(
            src_ref=src,
            dst_ref=dst,
            send_sem=sems.at[0],
            recv_sem=sems.at[1],
            device_id=where,
            device_id_type=MESH,
        )
        copy.start()

    def on_line(line, step):
        if line == 0:
            return ((z + step) % side) * side + y
        return z * side + (y + step) % side

    far_first = [2, 1, 3] if side == 4 else list(range(1, side))

    barrier = pltpu.get_barrier_semaphore()
    senders = [(section, on_line(line, d)) for line in range(2) for d in range(1, side)]
    senders += [(before, on_line(0, d)) for d in range(side)]
    senders += [(before, on_line(1, d)) for d in range(1, side)]
    for sender in senders:
        pl.semaphore_signal(barrier, inc=1, device_id=sender, device_id_type=MESH)
    smalls = [
        pltpu.make_async_copy(src, dst, load_sem.at[6 + i])
        for i, (src, dst) in enumerate(
            ((plan_hbm, plan), (gain_hbm, gain), (admissible_hbm, admissible))
        )
    ]
    for load in smalls:
        load.start()
    load_x = pltpu.make_async_copy(pending, x_raw, load_sem.at[0])
    load_x.start()
    loads = [
        pltpu.make_async_copy(
            w_in_hbm.at[j], w_in.at[:, pl.ds(j * HD, HD)], load_sem.at[1 + j]
        )
        for j in range(3)
    ]
    for load in loads:
        load.start()

    def columns(line, peer_at, q):
        block = peer_at * side + q if line == 0 else q * side + peer_at
        return w_out_hbm.at[:, pl.ds(pl.multiple_of(block * cols + line * LANES, LANES), LANES)]

    for line in range(2):
        for q in range(side):
            pltpu.make_async_copy(
                columns(line, place[line], q),
                w_line.at[line, place[line], :, pl.ds(q * LANES, LANES)],
                load_sem.at[4 + line],
            ).start()
    pl.semaphore_wait(barrier, len(senders))
    for step in far_first:
        for line in range(2):
            for q in range(side):
                send(
                    columns(line, (place[line] + step) % side, q),
                    w_line.at[line, place[line], :, pl.ds(q * LANES, LANES)],
                    wo_sem.at[line],
                    (section, on_line(line, step)),
                )
    for load in smalls:
        load.wait()
    lost = vanished[0]
    late_wrap = (lost == final - 1) | (lost == final - 2)
    load_x.wait()
    for c in range(count):
        for h in range(halves):
            for r in range(CHUNKS):
                start = c * cols + h * LANES
                block = x_raw[r * part : (r + 1) * part, start : start + LANES]
                x[0, r, h, c // side, c % side] = jnp.where(
                    section == lost, jnp.zeros_like(block), block
                )
    for load in loads:
        load.wait()

    def heads(k, r):
        def blocks():
            for c in range(count):
                for h in range(halves):
                    yield c * cols + h * LANES, x[k, r, h, c // side, c % side].astype(jnp.float32)

        summed = jnp.zeros((part, LANES), jnp.float32)
        for _, block in blocks():
            summed = summed + block
        mean = jnp.sum(summed, axis=-1, keepdims=True) * (1.0 / width)
        summed = jnp.zeros((part, LANES), jnp.float32)
        for _, block in blocks():
            block = block - mean
            summed = summed + block * block
        scale = lax.rsqrt(jnp.sum(summed, axis=-1, keepdims=True) * (1.0 / width) + NORM_EPS)
        for at, block in blocks():
            g = gain[:, at : at + LANES].astype(jnp.float32)
            normed[:, at : at + LANES] = ((block - mean) * scale * g).astype(jnp.bfloat16)
        projected = jnp.dot(normed[...], w_in[...], preferred_element_type=jnp.float32).astype(
            jnp.bfloat16
        )
        keys[r * part : (r + 1) * part, :] = projected[:, HD : 2 * HD]
        values[r * part : (r + 1) * part, :] = projected[:, 2 * HD :]
        seen = (r + 1) * part
        scores = lax.dot_general(
            projected[:, :HD],
            keys[:seen, :],
            (((1,), (1,)), ((), ())),
            preferred_element_type=jnp.float32,
        ) * HD ** (-0.5)
        row = lax.broadcasted_iota(jnp.int32, (part, seen), 0) + r * part
        col = lax.broadcasted_iota(jnp.int32, (part, seen), 1)
        scores = jnp.where(row >= col, scores, -jnp.inf)
        weights = jnp.exp(scores - jnp.max(scores, axis=-1, keepdims=True))
        probs = (weights / jnp.sum(weights, axis=-1, keepdims=True)).astype(jnp.bfloat16)
        mixed = jnp.dot(probs, values[:seen, :], preferred_element_type=jnp.float32)
        mixed = mixed.astype(jnp.bfloat16)
        for line in range(2):
            ctx[k, r, line, place[line]] = mixed
        for step in far_first:
            for line in range(2):
                block = ctx.at[k, r, line, place[line]]
                send(block, block, ctx_sem.at[k, r, line], (section, on_line(line, step)))

    def mix(k, r):
        early = (following == (lost + 2) % sections) & (lost <= final - 1)
        late = ((following == (lost + 3) % sections) & (lost <= final - 1)) | (
            (following == (lost + 4) % sections) & (lost <= final - 2)
        )
        enters = (k < 2) | ((k == 2) & late_wrap) | ((k == 3) & jnp.logical_not(late_wrap))
        enters = enters & (section == final)
        holds = (k == 2) & (lost == final) & (section == final)
        for line in range(2):
            arrive(ctx.at[k, r, line, pl.ds(0, side - 1)], ctx_sem.at[k, r, line, 1])
            context = jnp.concatenate([ctx[k, r, line, i] for i in range(side)], axis=1)
            branch = jnp.dot(
                context,
                w_line[line].reshape(side * HD, side * LANES),
                preferred_element_type=jnp.float32,
            )
            across = place[1 - line]
            for q in range(side):
                block = x[k, r, 0, z, q] if line == 0 else x[k, r, 1, q, y]
                share = branch[:, q * LANES : (q + 1) * LANES] + jnp.where(
                    across == q, block.astype(jnp.float32), 0.0
                )
                kept[k, r, line, q] = share.astype(jnp.bfloat16)

            @pl.when(k < SLOTS - 1)
            def _():
                entering = admissible[
                    plan[jnp.minimum(k, 2)],
                    r * part : (r + 1) * part,
                    line * LANES : (line + 1) * LANES,
                ]
                for q in range(side):
                    fresh = jnp.where(across == q, entering, jnp.zeros_like(entering))
                    value = jnp.where(holds, kept[0, r, line, q], kept[k, r, line, q])
                    sent[k, r, line, q] = jnp.where(enters, fresh, value)
                if line == 0:
                    for step in [*far_first, 0]:
                        send(
                            sent.at[k, r, 0],
                            got.at[k, r, 0, y],
                            part_sem.at[k, r, 0],
                            (following, on_line(1, step)),
                        )
                else:
                    for step in far_first:
                        send(
                            sent.at[k, r, 1],
                            got.at[k, r, 1, z],
                            part_sem.at[k, r, 1],
                            (section, on_line(0, step)),
                        )
                    for q in range(side):
                        got[k, r, 1, z, q] = sent[k, r, 1, q]

            @pl.when(k == SLOTS - 1)
            def _():
                for q in range(side):
                    value = jnp.where(late, kept[k, r, line, q], kept[3, r, line, q])
                    spare[r, line, q] = jnp.where(early, kept[1, r, line, q], value)
                for q in range(side):
                    send(
                        spare.at[r, line, q],
                        spare_got.at[r, line, across],
                        end_sem.at[r, line],
                        (following, z * side + q if line == 0 else q * side + y),
                    )

    def summed(k, r, line, q):
        value = got[k, r, line, 0, q].astype(jnp.float32)
        for i in range(1, side):
            value = value + got[k, r, line, i, q].astype(jnp.float32)
        return value.astype(jnp.bfloat16)

    def forward(k, r):
        arrive(got.at[k, r, 0], part_sem.at[k, r, 0, 1])
        for q in range(side):
            x[k + 1, r, 0, z, q] = summed(k, r, 0, q)
        for step in far_first:
            block = x.at[k + 1, r, 0, z]
            send(block, block, sum_sem.at[k, r, 0], (section, on_line(0, step)))
        arrive(got.at[k, r, 1, pl.ds(0, side - 1)], part_sem.at[k, r, 1, 1])
        for q in range(side):
            total[k, r, q] = summed(k, r, 1, q)
        for step in [*far_first, 0]:
            send(
                total.at[k, r],
                x.at[k + 1, r, 1, :, y],
                sum_sem.at[k, r, 1],
                (following, on_line(1, step)),
            )

    def gathered(k, r):
        arrive(x.at[k + 1, r, 0, pl.ds(0, side - 1)], sum_sem.at[k, r, 0, 1])
        arrive(x.at[k + 1, r, 1], sum_sem.at[k, r, 1, 1])

    def left(k):
        for r in range(CHUNKS):
            for line in range(2):
                arrive(ctx.at[k, r, line, pl.ds(0, side - 1)], ctx_sem.at[k, r, line, 0])
            arrive(got.at[k, r, 0], part_sem.at[k, r, 0, 0])
            arrive(got.at[k, r, 1, pl.ds(0, side - 1)], part_sem.at[k, r, 1, 0])
            arrive(x.at[k, r, 0, pl.ds(0, side - 1)], sum_sem.at[k, r, 0, 0])
            arrive(x.at[k, r, 1], sum_sem.at[k, r, 1, 0])

    def slot(k, carry):
        for r in range(CHUNKS):

            @pl.when(k > 0)
            def _():
                gathered(k - 1, r)

            heads(k, r)

        @pl.when(k == 0)
        def _():
            for line in range(2):
                arrive(w_line.at[line, 0], load_sem.at[4 + line])
                arrive(w_line.at[line, pl.ds(0, side - 1)], wo_sem.at[line, 1])

        @pl.when(k == SLOTS - 1)
        def _():
            for line in range(2):
                arrive(w_line.at[line, pl.ds(0, side - 1)], wo_sem.at[line, 0])
            behind = (section > lost) & (section <= lost + 3)
            newest = jnp.where(section == 0, jnp.logical_not(late_wrap), behind)
            for c in range(count):
                for h in range(halves):
                    for r in range(CHUNKS):
                        at = (r, h, c // side, c % side)
                        block = jnp.where(newest, x[SLOTS - 1, *at], x[SLOTS - 2, *at])
                        block = jnp.where(section == lost, jnp.zeros_like(block), block)
                        start = c * cols + h * LANES
                        out_ref[r * part : (r + 1) * part, start : start + LANES] = block

        @pl.when(k > 0)
        def _():
            left(k - 1)

        for r in range(CHUNKS):
            mix(k, r)

        @pl.when(k < SLOTS - 1)
        def _():
            for r in range(CHUNKS):
                forward(k, r)

        return carry

    lax.fori_loop(0, SLOTS, slot, 0)

    for r in range(CHUNKS):
        for line in range(2):
            arrive(spare_got.at[r, line], end_sem.at[r, line, 1])
            value = spare_got[r, line, 0].astype(jnp.float32)
            for i in range(1, side):
                value = value + spare_got[r, line, i].astype(jnp.float32)
            standby_ref[r * part : (r + 1) * part, line * LANES : (line + 1) * LANES] = (
                value.astype(jnp.bfloat16)
            )
    for r in range(CHUNKS):
        for line in range(2):
            arrive(ctx.at[SLOTS - 1, r, line, pl.ds(0, side - 1)], ctx_sem.at[SLOTS - 1, r, line, 0])
            arrive(spare.at[r, line], end_sem.at[r, line, 0])


def in_hbm(array):
    return pltpu.with_memory_space_constraint(array, pltpu.HBM)


def per_device(pending, admissible, plan, vanished_hop, w_in, w_out, gain):
    count = lax.axis_size("tp")
    side = int(round(count**0.5))
    rows, width = pending.shape[1:]
    cols = width // count
    part = rows // CHUNKS
    halves = cols // LANES
    vmem = pl.BlockSpec(memory_space=pltpu.VMEM)
    smem = pl.BlockSpec(memory_space=pltpu.SMEM)
    hbm = pl.BlockSpec(memory_space=pltpu.HBM)
    bf16 = jnp.bfloat16
    dma = pltpu.SemaphoreType.DMA
    out, standby = pl.pallas_call(
        functools.partial(kernel, side),
        out_shape=(
            jax.ShapeDtypeStruct((rows, width), bf16),
            jax.ShapeDtypeStruct((rows, cols), bf16),
        ),
        in_specs=[hbm] * 3 + [smem] + [hbm] * 3,
        out_specs=(vmem, vmem),
        scratch_shapes=[
            pltpu.VMEM((rows, width), bf16),
            pltpu.VMEM((width, 3 * HD), bf16),
            pltpu.VMEM((2, side, HD, side * LANES), bf16),
            pltpu.VMEM((SLOTS, CHUNKS, halves, side, side, part, LANES), bf16),
            pltpu.VMEM((SLOTS, CHUNKS, 2, side, part, HD), bf16),
            pltpu.VMEM((SLOTS, CHUNKS, 2, side, part, LANES), bf16),
            pltpu.VMEM((SLOTS - 1, CHUNKS, 2, side, part, LANES), bf16),
            pltpu.VMEM((SLOTS - 1, CHUNKS, 2, side, side, part, LANES), bf16),
            pltpu.VMEM((SLOTS - 1, CHUNKS, side, part, LANES), bf16),
            pltpu.VMEM((part, width), bf16),
            pltpu.VMEM((rows, HD), bf16),
            pltpu.VMEM((rows, HD), bf16),
            pltpu.VMEM((CHUNKS, 2, side, part, LANES), bf16),
            pltpu.VMEM((CHUNKS, 2, side, part, LANES), bf16),
            pltpu.VMEM(admissible.shape, bf16),
            pltpu.VMEM(gain.shape, bf16),
            pltpu.SMEM(plan.shape, jnp.int32),
            dma((9,)),
            dma((2, 2)),
            dma((SLOTS, CHUNKS, 2, 2)),
            dma((SLOTS - 1, CHUNKS, 2, 2)),
            dma((SLOTS - 1, CHUNKS, 2, 2)),
            dma((CHUNKS, 2, 2)),
        ],
        compiler_params=pltpu.CompilerParams(
            has_side_effects=True, vmem_limit_bytes=48 * 1024 * 1024, collective_id=0
        ),
        name="relay",
    )(
        in_hbm(pending[0]),
        in_hbm(admissible),
        in_hbm(plan),
        vanished_hop,
        in_hbm(jnp.moveaxis(w_in[0], 1, 0)),
        in_hbm(w_out[0]),
        in_hbm(gain),
    )
    return out[None], standby[None]


def solution(mesh):
    placed = (
        P("section", None, None),
        P(None, None, "tp"),
        P(),
        P(),
        P("section", None, None, "tp"),
        P("section", "tp", None),
        P("section", None),
    )
    return jax.shard_map(
        per_device,
        mesh=mesh,
        in_specs=placed,
        out_specs=(P("section", None, None), P("section", None, "tp")),
        check_vma=False,
    )
```

time: 97.7 us -> 93.6 us (0.958)
  Pallas kernels: 94.7 us -> 90.6 us
    pallas_call x1, Pallas kernels: 94.7 us -> 90.6 us  [per_device(): pl.pallas_call(functools.partial(kernel, side), out_shape=(jax.ShapeDtype...]
where the time goes in v5:
time: 93.6 us; the launch traced here: 93.5 us
  Pallas kernels  90.6 us (97%)
  local copies, waits for them, and re-layouts  1.6 us (2%)
  between operations  1.29 us (1%)
    pallas_call x1, Pallas kernels, per_device(): pl.pallas_call(functools.partial(kernel, side), out_shape=(jax.ShapeDtype...  90.6 us

profile of v5, /device:TPU:1, one launch (start us, length us, event | category | flops | bytes accessed | tf_op | source)
XLA Modules:
  0.0 93.5 jit_solution(590550398889164919)
XLA Ops:
  1.3 90.6 %relay.1 = (bf16[128,4096]{1,0:T(8,128)(2,1)S(1)}, bf16[128,256]{1,0:T(8,128)(2,1)S(1)}) custom-call(bf16[128,4096]{1,0:T(8,128)(2,1)} %bitcast.10, bf16[4,128,256]{2,1,0:T(8,128)(2,1)} %admissible_hbm.1, s32[4]{0:T(128)} %plan_hbm.1, s32[1]{0:T(128)S(6)} %copy.11.vanished, bf16[3,4096,128]{2,1,0:T(8,128)(2,1)} %bitcast.9, bf16[128,4096]{1,0:T(8,128)(2,1)} %bitcast.11, ...), custom_call_target="tpu_custom_call" | custom-call | tf_op jit(solution)/shard_map/relay/pallas_call | solution.py:376
  91.9 1.0 %copy.12 = bf16[1,128,4096]{2,1,0:T(8,128)(2,1)} copy(bf16[1,128,4096]{2,1,0:T(8,128)(2,1)S(1)} %bitcast.7) | data formatting | bytes 2097152
  92.9 0.6 copy.13

commit v6 on v5

--- a/solution.py
+++ b/solution.py
@@ -266,12 +266,6 @@
         return value.astype(jnp.bfloat16)
 
     def forward(k, r):
-        arrive(got.at[k, r, 0], part_sem.at[k, r, 0, 1])
-        for q in range(side):
-            x[k + 1, r, 0, z, q] = summed(k, r, 0, q)
-        for step in far_first:
-            block = x.at[k + 1, r, 0, z]
-            send(block, block, sum_sem.at[k, r, 0], (section, on_line(0, step)))
         arrive(got.at[k, r, 1, pl.ds(0, side - 1)], part_sem.at[k, r, 1, 1])
         for q in range(side):
             total[k, r, q] = summed(k, r, 1, q)
@@ -282,6 +276,12 @@
                 sum_sem.at[k, r, 1],
                 (following, on_line(1, step)),
             )
+        arrive(got.at[k, r, 0], part_sem.at[k, r, 0, 1])
+        for q in range(side):
+            x[k + 1, r, 0, z, q] = summed(k, r, 0, q)
+        for step in far_first:
+            block = x.at[k + 1, r, 0, z]
+            send(block, block, sum_sem.at[k, r, 0], (section, on_line(0, step)))
 
     def gathered(k, r):
         arrive(x.at[k + 1, r, 0, pl.ds(0, side - 1)], sum_sem.at[k, r, 0, 1])

time: 93.6 us -> 93.2 us (level)
  no operation moved by 1% of the time
where the time goes in v6:
time: 93.2 us; the launch traced here: 93 us
  Pallas kernels  90.2 us (97%)
  local copies, waits for them, and re-layouts  1.6 us (2%)
  between operations  1.29 us (1%)
    pallas_call x1, Pallas kernels, per_device(): pl.pallas_call(functools.partial(kernel, side), out_shape=(jax.ShapeDtype...  90.2 us

profile of v6, /device:TPU:1, one launch (start us, length us, event | category | flops | bytes accessed | tf_op | source)
XLA Modules:
  0.0 93.0 jit_solution(5095255671712820337)
XLA Ops:
  1.3 90.2 %relay.1 = (bf16[128,4096]{1,0:T(8,128)(2,1)S(1)}, bf16[128,256]{1,0:T(8,128)(2,1)S(1)}) custom-call(bf16[128,4096]{1,0:T(8,128)(2,1)} %bitcast.10, bf16[4,128,256]{2,1,0:T(8,128)(2,1)} %admissible_hbm.1, s32[4]{0:T(128)} %plan_hbm.1, s32[1]{0:T(128)S(6)} %copy.11.vanished, bf16[3,4096,128]{2,1,0:T(8,128)(2,1)} %bitcast.9, bf16[128,4096]{1,0:T(8,128)(2,1)} %bitcast.11, ...), custom_call_target="tpu_custom_call" | custom-call | tf_op jit(solution)/shard_map/relay/pallas_call | solution.py:376
  91.4 1.0 %copy.12 = bf16[1,128,4096]{2,1,0:T(8,128)(2,1)} copy(bf16[1,128,4096]{2,1,0:T(8,128)(2,1)S(1)} %bitcast.7) | data formatting | bytes 2097152
  92.4 0.6 copy.13
